TPU v7x, 32 devices: a whole 2x2x4 slice. The times are simulated.
32 devices in a mesh: dp: 4 (over y, x), expert: 8 (over z, core).
Axes of the slice: x: 2, y: 2, z: 4, core: 2. Of those that a mesh axis runs over, the one named last changes fastest.
Arguments:
- tokens: bfloat16 [16384, 2048], P(('dp', 'expert')), may hold values from -6 to 6
- expert_ids: int32 [16384, 1], P(('dp', 'expert')), may hold values from 0 to 7; in each aligned block of 512 rows (0 to 511, 512 to 1023, ...) at most 128 rows name the same one
- gate_proj: bfloat16 [8, 2048, 768], P('expert'), may hold values from -0.125 to 0.125
- up_proj: bfloat16 [8, 2048, 768], P('expert'), may hold values from -0.125 to 0.125
- down_proj: bfloat16 [8, 768, 2048], P('expert'), may hold values from -0.21875 to 0.21875
Outputs:
- mixed: bfloat16 [16384, 2048], P(('dp', 'expert'))
- slot_index: int32 [16384], P(('dp', 'expert'))
Inputs may be any that keep to these rules, and one draw needn't show every extreme that they name: `expert_ids`: among the rows of one device no expert is named more than 128 times; in some devices' rows one expert is named exactly 128 times.
All inputs are finite; a program needn't handle non-finite values.
Results may differ from a plain program's by a relative error of at most 0.0046.
The roundings to bfloat16 on the way count: a program that leaves them out, or rounds other values in their place, can miss the bound.
Values may be sent and summed in bfloat16 or wider, within the bound.
A program may use at most 64 MiB of HBM per device.

v0:
```python
import functools

import jax
import jax.numpy as jnp
from jax import lax
from jax.experimental import pallas as pl
from jax.experimental.pallas import tpu as pltpu
from jax.sharding import PartitionSpec as P

MESH = pl.DeviceIdType.MESH
F32 = jnp.float32
BF16 = jnp.bfloat16
LANES = 128


def spread(step, n):
    half = (step // 2) * (2 * (step % 2) - 1)
    return jnp.where(step == 0, 0, n // 2 + half)


def direct_kernel(
    n, dps, most, capacity,
    row_ids, col_ids, tok_ref, gate_hbm, up_hbm, down_hbm,
    out_ref, slot_ref,
    gate_ref, up_ref, down_ref, outgoing, arrived, results, returned,
    position, offset, counts, count_all, totals, total_all,
    weight_sem, go_send, go_recv, back_send, back_recv,
    count_send, count_recv, total_send, total_recv,
):
    me = lax.axis_index("expert")
    group = lax.axis_index("dp")
    tok = tok_ref.shape[0]
    width = tok_ref.shape[1]

    weights = [
        pltpu.make_async_copy(src.at[0], dst, weight_sem.at[i])
        for i, (src, dst) in enumerate(
            ((gate_hbm, gate_ref), (up_hbm, up_ref), (down_hbm, down_ref))
        )
    ]
    for copy in weights:
        copy.start()

    barrier = pltpu.get_barrier_semaphore()

    def greet(i, c):
        pl.semaphore_signal(
            barrier, inc=1, device_id={"expert": lax.rem(me + i, n)}, device_id_type=MESH
        )
        return c

    def greet_dp(i, c):
        pl.semaphore_signal(
            barrier, inc=1, device_id={"dp": lax.rem(group + i, dps)}, device_id_type=MESH
        )
        return c

    lax.fori_loop(1, n, greet, 0)
    lax.fori_loop(1, dps, greet_dp, 0)

    earlier = lax.broadcasted_iota(jnp.int32, (tok, tok), 0) < lax.broadcasted_iota(
        jnp.int32, (tok, tok), 1
    )
    later = lax.broadcasted_iota(jnp.int32, (tok, tok), 0) > lax.broadcasted_iota(
        jnp.int32, (tok, tok), 1
    )
    ids_row = row_ids[...]
    hot_row = (ids_row == lax.broadcasted_iota(jnp.int32, (n, tok), 0)).astype(F32)
    before_row = jnp.dot(
        hot_row.astype(BF16), earlier.astype(F32).astype(BF16), preferred_element_type=F32
    )
    rank_row = jnp.sum(before_row * hot_row, axis=0, keepdims=True).astype(jnp.int32)
    pos_row = ids_row * most + rank_row
    counts[...] = jnp.broadcast_to(
        jnp.sum(hot_row, axis=1, keepdims=True), (n, LANES)
    ).astype(jnp.int32)

    ids_col = col_ids[...]
    hot_col = (ids_col == lax.broadcasted_iota(jnp.int32, (tok, n), 1)).astype(F32)
    before_col = jnp.dot(
        later.astype(F32).astype(BF16), hot_col.astype(BF16), preferred_element_type=F32
    )
    rank_col = jnp.sum(before_col * hot_col, axis=1, keepdims=True).astype(jnp.int32)
    position[...] = ids_col * most + rank_col

    def go(dest, source):
        return pltpu.make_async_remote_copy(
            src_ref=outgoing.at[dest], dst_ref=arrived.at[source],
            send_sem=go_send.at[dest], recv_sem=go_recv.at[source],
            device_id={"expert": dest}, device_id_type=MESH,
        )

    def back(dest, source):
        return pltpu.make_async_remote_copy(
            src_ref=results.at[dest], dst_ref=returned.at[source],
            send_sem=back_send.at[dest], recv_sem=back_recv.at[source],
            device_id={"expert": dest}, device_id_type=MESH,
        )

    def count(dest, source):
        return pltpu.make_async_remote_copy(
            src_ref=counts, dst_ref=count_all.at[source],
            send_sem=count_send.at[dest], recv_sem=count_recv.at[source],
            device_id={"expert": dest}, device_id_type=MESH,
        )

    def total(dest, source):
        return pltpu.make_async_remote_copy(
            src_ref=totals, dst_ref=total_all.at[source],
            send_sem=total_send.at[dest], recv_sem=total_recv.at[source],
            device_id={"dp": dest}, device_id_type=MESH,
        )

    def pack(dest):
        pick = (
            lax.broadcasted_iota(jnp.int32, (most, tok), 0) + dest * most == pos_row
        ).astype(F32).astype(BF16)
        return jnp.dot(pick, tok_ref[...], preferred_element_type=F32).astype(BF16)

    pl.semaphore_wait(barrier, n + dps - 2)

    def dispatch(i, c):
        dest = lax.rem(me + spread(i, n), n)
        outgoing[dest] = pack(dest)
        go(dest, me).start()
        return c

    lax.fori_loop(1, n, dispatch, 0)

    def tell(i, c):
        count(lax.rem(me + i, n), me).start()
        return c

    lax.fori_loop(1, n, tell, 0)
    count_all[me] = counts[...]
    arrived[me] = pack(me)

    for copy in weights:
        copy.wait()

    def ffn(source):
        rows = arrived[source]
        gate = jnp.dot(rows, gate_ref[...], preferred_element_type=F32)
        up = jnp.dot(rows, up_ref[...], preferred_element_type=F32)
        hidden = (gate / (1.0 + jnp.exp(-gate)) * up).astype(BF16)
        return jnp.dot(hidden, down_ref[...], preferred_element_type=F32).astype(BF16)

    def expert_step(i, c):
        source = lax.rem(me + n - spread(i, n), n)

        @pl.when(i > 0)
        def _():
            go(me, source).wait_recv()

        results[source] = ffn(source)

        @pl.when(i > 0)
        def _():
            back(source, me).start()

        return c

    lax.fori_loop(0, n, expert_step, 0)

    def heard(i, c):
        count(me, lax.rem(me + i, n)).wait_recv()
        return c

    lax.fori_loop(1, n, heard, 0)

    def add(i, carry):
        inner, whole = carry
        here = count_all[i]
        return inner + here * (i < me).astype(jnp.int32), whole + here

    zero = jnp.zeros((n, LANES), jnp.int32)
    inner, whole = lax.fori_loop(0, n, add, (zero, zero))
    totals[...] = whole

    def tell_dp(i, c):
        total(lax.rem(group + i, dps), group).start()
        return c

    lax.fori_loop(1, dps, tell_dp, 0)
    total_all[group] = whole

    def heard_dp(i, c):
        total(group, lax.rem(group + i, dps)).wait_recv()
        return c

    lax.fori_loop(1, dps, heard_dp, 0)

    def add_dp(i, outer):
        return outer + total_all[i] * (i < group).astype(jnp.int32)

    offset[...] = inner + lax.fori_loop(0, dps, add_dp, zero)
    slot_ref[...] = (
        jnp.sum(
            hot_row * offset[:, 0:1].astype(F32), axis=0, keepdims=True
        ).astype(jnp.int32)
        + rank_row
    )

    piece = min(width, 512)

    def combine(source, block, first):
        lane = lax.broadcasted_iota(jnp.int32, (tok, most), 1)
        fits = offset[pl.ds(source, 1), 0:most] + lax.broadcasted_iota(
            jnp.int32, (1, most), 1
        ) < capacity
        pick = (lane + source * most == position[...]) & fits
        pick = pick.astype(F32).astype(BF16)
        for at in range(0, width, piece):
            part = jnp.dot(
                pick, block[source, :, at : at + piece], preferred_element_type=F32
            ).astype(BF16)
            if first:
                out_ref[:, at : at + piece] = part
            else:
                out_ref[:, at : at + piece] += part

    combine(me, results, True)

    def combine_step(i, c):
        source = lax.rem(me + n - spread(i, n), n)
        back(me, source).wait_recv()
        combine(source, returned, False)
        return c

    lax.fori_loop(1, n, combine_step, 0)

    def drain(i, c):
        other = lax.rem(me + i, n)
        go(other, me).wait_send()
        back(other, me).wait_send()
        count(other, me).wait_send()
        return c

    lax.fori_loop(1, n, drain, 0)

    def drain_dp(i, c):
        total(lax.rem(group + i, dps), group).wait_send()
        return c

    lax.fori_loop(1, dps, drain_dp, 0)


def direct(tokens, expert_ids, gate_proj, up_proj, down_proj):
    tok, width = tokens.shape
    hidden = gate_proj.shape[2]
    n = lax.axis_size("expert")
    dps = lax.axis_size("dp")
    most = 2 * tok // n
    capacity = tok * dps
    vmem = pl.BlockSpec(memory_space=pltpu.VMEM)
    anywhere = pl.BlockSpec(memory_space=pltpu.MemorySpace.HBM)
    dma = pltpu.SemaphoreType.DMA
    block = pltpu.VMEM((n, most, width), BF16)
    mixed, slot = pl.pallas_call(
        functools.partial(direct_kernel, n, dps, most, capacity),
        out_shape=(
            jax.ShapeDtypeStruct((tok, width), BF16),
            jax.ShapeDtypeStruct((1, tok), jnp.int32),
        ),
        in_specs=[vmem, vmem, vmem, anywhere, anywhere, anywhere],
        out_specs=(vmem, vmem),
        scratch_shapes=[
            pltpu.VMEM((width, hidden), BF16),
            pltpu.VMEM((width, hidden), BF16),
            pltpu.VMEM((hidden, width), BF16),
            block, block, block, block,
            pltpu.VMEM((tok, 1), jnp.int32),
            pltpu.VMEM((n, LANES), jnp.int32),
            pltpu.VMEM((n, LANES), jnp.int32),
            pltpu.VMEM((n, n, LANES), jnp.int32),
            pltpu.VMEM((n, LANES), jnp.int32),
            pltpu.VMEM((dps, n, LANES), jnp.int32),
            dma((3,)), dma((n,)), dma((n,)), dma((n,)), dma((n,)),
            dma((n,)), dma((n,)), dma((dps,)), dma((dps,)),
        ],
        compiler_params=pltpu.CompilerParams(
            collective_id=0, has_side_effects=True, vmem_limit_bytes=60 * 2**20
        ),
    )(
        expert_ids.reshape(1, tok), expert_ids, tokens, gate_proj, up_proj, down_proj
    )
    return mixed, slot.reshape(tok)


def entering(part, axis, combine, identity):
    place = lax.axis_index(axis)
    gathered = lax.all_gather(part, axis)
    state = jnp.zeros_like(part) + jnp.asarray(identity, part.dtype)

    def one(hop, state):
        return combine(state, lax.dynamic_index_in_dim(gathered, hop, 0, False))

    return lax.fori_loop(0, place, one, state)


def add_counts(earlier, later):
    return earlier + later


def expert_ffn(rows, gate_proj, up_proj, down_proj):
    gate_val = jnp.dot(rows, gate_proj[0], preferred_element_type=jnp.float32)
    up_val = jnp.dot(rows, up_proj[0], preferred_element_type=jnp.float32)
    hidden = (jax.nn.silu(gate_val) * up_val).astype(jnp.bfloat16)
    return jnp.dot(hidden, down_proj[0], preferred_element_type=jnp.float32).astype(jnp.bfloat16)


def padded(tokens, expert_ids, gate_proj, up_proj, down_proj):
    tok_rows, width = tokens.shape
    experts_all = lax.axis_size("expert")
    most = 2 * tok_rows // experts_all
    capacity = tok_rows * lax.axis_size("dp")
    choices = expert_ids[:, 0]
    onehot = (choices[:, None] == jnp.arange(experts_all, dtype=jnp.int32)[None, :]).astype(
        jnp.int32
    )
    counts = jnp.sum(onehot, axis=0)
    inner = entering(counts, "expert", add_counts, jnp.zeros_like(counts))
    totals = lax.psum(counts, "expert")
    outer = entering(totals, "dp", add_counts, jnp.zeros_like(totals))
    offset = inner + outer
    before = jnp.cumsum(onehot, axis=0) - onehot
    local_rank = jnp.sum(before * onehot, axis=1)
    global_slot = (jnp.sum(onehot * offset[None, :], axis=1) + local_rank).astype(jnp.int32)
    is_kept = global_slot < capacity
    position = choices * most + local_rank
    targets = jnp.arange(experts_all * most, dtype=jnp.int32)
    dispatch = ((targets[:, None] == position[None, :]) & is_kept[None, :]).astype(jnp.bfloat16)
    outgoing = jnp.dot(dispatch, tokens, preferred_element_type=jnp.float32).astype(jnp.bfloat16)
    outgoing = outgoing.reshape(experts_all, most, width)
    arrived = lax.all_to_all(outgoing, "expert", split_axis=0, concat_axis=0, tiled=True)
    sources, slots_here, _ = arrived.shape
    flat = arrived.reshape(sources * slots_here, width)
    returned = lax.all_to_all(
        expert_ffn(flat, gate_proj, up_proj, down_proj).reshape(sources, slots_here, width),
        "expert",
        split_axis=0,
        concat_axis=0,
        tiled=True,
    )
    flat_back = returned.reshape(experts_all * most, width)
    mixed = lax.dot_general(
        dispatch, flat_back, (((0,), (0,)), ((), ())), preferred_element_type=jnp.float32
    )
    return (mixed.astype(jnp.bfloat16), global_slot)


def relay_kernel(
    n, dps, most, base, dense, capacity,
    row_ids, col_ids, tok_ref, gate_hbm, up_hbm, down_hbm,
    out_ref, slot_ref, flag_ref,
    gate_ref, up_ref, down_ref, outgoing, arrived, results, returned,
    x_out, x_in, x_back, x_home, relay_out, relay_in,
    position, x_position, offset, x_first, x_size, r_first, r_size,
    counts, count_all, totals, total_all,
    weight_sem, go_send, go_recv, back_send, back_recv,
    over_send, over_recv, gather_send, gather_recv, x_send, x_recv,
    count_send, count_recv, total_send, total_recv,
):
    me = lax.axis_index("expert")
    group = lax.axis_index("dp")
    tok, width = tok_ref.shape
    hn = n // 2
    over = most - base
    near = lax.div(me, hn) * hn
    far = hn - near
    place = me - near
    partner = far + place
    piece = min(width, 512)

    def around(i):
        return lax.rem(place + i, hn)

    weights = [
        pltpu.make_async_copy(src.at[0], dst, weight_sem.at[i])
        for i, (src, dst) in enumerate(
            ((gate_hbm, gate_ref), (up_hbm, up_ref), (down_hbm, down_ref))
        )
    ]
    for copy in weights:
        copy.start()

    barrier = pltpu.get_barrier_semaphore()

    def greet(i, c):
        pl.semaphore_signal(
            barrier, inc=1, device_id={"expert": lax.rem(me + i, n)}, device_id_type=MESH
        )
        return c

    def greet_dp(i, c):
        pl.semaphore_signal(
            barrier, inc=1, device_id={"dp": lax.rem(group + i, dps)}, device_id_type=MESH
        )
        return c

    lax.fori_loop(1, n, greet, 0)
    lax.fori_loop(1, dps, greet_dp, 0)

    def iota(shape, axis):
        return lax.broadcasted_iota(jnp.int32, shape, axis)

    def ones(mask):
        return mask.astype(F32).astype(BF16)

    def dot(a, b):
        return jnp.dot(a, b, preferred_element_type=F32)

    def excess(count, half):
        rows = iota((n, LANES), 0)
        inside = (rows >= half) & (rows < half + hn)
        size = jnp.where(inside, jnp.maximum(count - base, 0), 0)
        first = dot(
            ones(iota((n, n), 1) < iota((n, n), 0)), size.astype(F32).astype(BF16)
        ).astype(jnp.int32)
        return first, size

    ids_row = row_ids[...]
    hot_row = (ids_row == iota((n, tok), 0)).astype(F32)
    before_row = dot(hot_row.astype(BF16), ones(iota((tok, tok), 0) < iota((tok, tok), 1)))
    rank_row = jnp.sum(before_row * hot_row, axis=0, keepdims=True).astype(jnp.int32)
    pos_row = ids_row * most + rank_row
    mine = jnp.broadcast_to(
        jnp.sum(hot_row, axis=1, keepdims=True), (n, LANES)
    ).astype(jnp.int32)
    counts[...] = mine
    first, size = excess(mine, far)
    x_first[...] = first
    x_size[...] = size
    start_row = jnp.sum(
        hot_row * x_first[:, 0:1].astype(F32), axis=0, keepdims=True
    ).astype(jnp.int32)
    x_row = jnp.where(
        (ids_row >= far) & (ids_row < far + hn) & (rank_row >= base),
        start_row + rank_row - base, -1,
    )

    ids_col = col_ids[...]
    hot_col = (ids_col == iota((tok, n), 1)).astype(F32)

    def go(dest, source, far_off):
        rows = pl.ds(0, base if far_off else most)
        return pltpu.make_async_remote_copy(
            src_ref=outgoing.at[dest, rows], dst_ref=arrived.at[source, rows],
            send_sem=go_send.at[dest], recv_sem=go_recv.at[source],
            device_id={"expert": dest}, device_id_type=MESH,
        )

    def back(dest, source, far_off):
        rows = pl.ds(0, base if far_off else most)
        return pltpu.make_async_remote_copy(
            src_ref=results.at[dest, rows], dst_ref=returned.at[source, rows],
            send_sem=back_send.at[dest], recv_sem=back_recv.at[source],
            device_id={"expert": dest}, device_id_type=MESH,
        )

    def forward(dest, slot, source):
        return pltpu.make_async_remote_copy(
            src_ref=relay_out.at[slot], dst_ref=arrived.at[source, pl.ds(base, over)],
            send_sem=over_send.at[slot], recv_sem=over_recv.at[source],
            device_id={"expert": dest}, device_id_type=MESH,
        )

    def gather(dest, source, slot):
        return pltpu.make_async_remote_copy(
            src_ref=results.at[source, pl.ds(base, over)], dst_ref=relay_in.at[slot],
            send_sem=gather_send.at[source], recv_sem=gather_recv.at[slot],
            device_id={"expert": dest}, device_id_type=MESH,
        )

    def cross(which, src, dst):
        return pltpu.make_async_remote_copy(
            src_ref=src, dst_ref=dst,
            send_sem=x_send.at[which], recv_sem=x_recv.at[which],
            device_id={"expert": partner}, device_id_type=MESH,
        )

    def count(dest, source):
        return pltpu.make_async_remote_copy(
            src_ref=counts, dst_ref=count_all.at[source],
            send_sem=count_send.at[dest], recv_sem=count_recv.at[source],
            device_id={"expert": dest}, device_id_type=MESH,
        )

    def total(dest, source):
        return pltpu.make_async_remote_copy(
            src_ref=totals, dst_ref=total_all.at[source],
            send_sem=total_send.at[dest], recv_sem=total_recv.at[source],
            device_id={"dp": dest}, device_id_type=MESH,
        )

    def pack(dest, rows):
        pick = ones(iota((rows, tok), 0) + dest * most == pos_row)
        return dot(pick, tok_ref[...]).astype(BF16)

    x_out[...] = dot(ones(iota((dense, tok), 0) == x_row), tok_ref[...]).astype(BF16)

    pl.semaphore_wait(barrier, n + dps - 2)

    def tell(i, c):
        count(lax.rem(me + i, n), me).start()
        return c

    lax.fori_loop(1, n, tell, 0)
    send_x = cross(0, x_out, x_in)
    send_x.start()

    def dispatch_near(i, c):
        dest = near + around(i)
        outgoing[dest] = pack(dest, most)
        go(dest, me, False).start()
        return c

    lax.fori_loop(1, hn, dispatch_near, 0)

    def dispatch_far(i, c):
        dest = far + around(i)
        outgoing[dest, pl.ds(0, base)] = pack(dest, base)
        go(dest, me, True).start()
        return c

    lax.fori_loop(0, hn, dispatch_far, 0)
    count_all[me] = mine
    arrived[me] = pack(me, most)

    before_col = dot(ones(iota((tok, tok), 0) > iota((tok, tok), 1)), hot_col.astype(BF16))
    rank_col = jnp.sum(before_col * hot_col, axis=1, keepdims=True).astype(jnp.int32)
    position[...] = ids_col * most + rank_col
    lane = iota((1, n), 1)
    size_lane = jnp.where(
        (lane >= far) & (lane < far + hn),
        jnp.maximum(jnp.sum(hot_col, axis=0, keepdims=True) - base, 0.0), 0.0,
    )
    first_lane = dot(
        jnp.broadcast_to(size_lane, (16, n)).astype(BF16),
        ones(iota((n, n), 0) < iota((n, n), 1)),
    )[0:1]
    start_col = jnp.sum(hot_col * first_lane, axis=1, keepdims=True).astype(jnp.int32)
    x_position[...] = jnp.where(
        (ids_col >= far) & (ids_col < far + hn) & (rank_col >= base),
        start_col + rank_col - base, -1,
    )

    for copy in weights:
        copy.wait()

    def ffn(source):
        rows = arrived[source]
        gate = dot(rows, gate_ref[...])
        up = dot(rows, up_ref[...])
        hidden = (gate / (1.0 + jnp.exp(-gate)) * up).astype(BF16)
        results[source] = dot(hidden, down_ref[...]).astype(BF16)

    def near_step(i, c):
        source = near + lax.rem(place + hn - i, hn)

        @pl.when(i > 0)
        def _():
            go(me, source, False).wait_recv()

        ffn(source)

        @pl.when(i > 0)
        def _():
            back(source, me, False).start()

        @pl.when(i == 0)
        def _():
            unpack()

        return c

    def unpack():
        count(me, partner).wait_recv()
        send_x.wait_recv()
        first, size = excess(count_all[partner], near)
        r_first[...] = first
        r_size[...] = size

        def one(i, c):
            slot = around(i)
            dest = near + slot
            row = iota((over, dense), 0)
            pick = (iota((over, dense), 1) == row + r_first[pl.ds(dest, 1), 0:1]) & (
                row < r_size[pl.ds(dest, 1), 0:1]
            )
            block = dot(ones(pick), x_in[...]).astype(BF16)

            @pl.when(i == 0)
            def _():
                arrived[partner, pl.ds(base, over)] = block

            @pl.when(i > 0)
            def _():
                relay_out[slot] = block
                forward(dest, slot, partner).start()

            return c

        lax.fori_loop(0, hn, one, 0)

    lax.fori_loop(0, hn, near_step, 0)

    def far_step(i, c):
        slot = lax.rem(place + hn - i, hn)
        source = far + slot
        go(me, source, True).wait_recv()

        @pl.when(i > 0)
        def _():
            forward(me, place, source).wait_recv()

        ffn(source)
        back(source, me, True).start()

        @pl.when(i > 0)
        def _():
            gather(near + slot, source, place).start()

        @pl.when(i == 0)
        def _():
            relay_in[place] = results[source, pl.ds(base, over)]

        return c

    lax.fori_loop(0, hn, far_step, 0)

    def collect(i, c):
        gather(me, partner, around(i)).wait_recv()
        return c

    lax.fori_loop(1, hn, collect, 0)
    picks = []
    for slot in range(hn):
        column = iota((dense, over), 1)
        pick = (
            iota((dense, over), 0) == column + r_first[pl.ds(near + slot, 1), 0:1]
        ) & (column < r_size[pl.ds(near + slot, 1), 0:1])
        picks.append(ones(pick))
    for at in range(0, width, piece):
        acc = dot(picks[0], relay_in[0, :, at : at + piece])
        for slot in range(1, hn):
            acc += dot(picks[slot], relay_in[slot, :, at : at + piece])
        x_back[:, at : at + piece] = acc.astype(BF16)
    send_back = cross(1, x_back, x_home)
    send_back.start()

    def heard(i, c):
        @pl.when(i != hn)
        def _():
            count(me, lax.rem(me + i, n)).wait_recv()

        return c

    lax.fori_loop(1, n, heard, 0)

    def add(i, carry):
        inner, whole, need = carry
        here = count_all[i]
        other = hn - lax.div(i, hn) * hn
        rows = iota((n, LANES), 0)
        outside = (rows >= other) & (rows < other + hn)
        extra = jnp.sum(
            jnp.where(outside, jnp.maximum(here - base, 0), 0), axis=0, keepdims=True
        )
        return (
            inner + here * (i < me).astype(jnp.int32), whole + here, jnp.maximum(need, extra)
        )

    zero = jnp.zeros((n, LANES), jnp.int32)
    inner, whole, need = lax.fori_loop(
        0, n, add, (zero, zero, jnp.zeros((1, LANES), jnp.int32))
    )
    need = jnp.broadcast_to(need, (8, LANES))
    totals[0] = whole
    totals[1] = need

    def tell_dp(i, c):
        total(lax.rem(group + i, dps), group).start()
        return c

    lax.fori_loop(1, dps, tell_dp, 0)
    total_all[group, 0] = whole
    total_all[group, 1] = need

    def heard_dp(i, c):
        total(group, lax.rem(group + i, dps)).wait_recv()
        return c

    lax.fori_loop(1, dps, heard_dp, 0)

    def add_dp(i, carry):
        outer, most_needed = carry
        return (
            outer + total_all[i, 0] * (i < group).astype(jnp.int32),
            jnp.maximum(most_needed, total_all[i, 1]),
        )

    outer, needed = lax.fori_loop(0, dps, add_dp, (zero, need))
    offset[...] = inner + outer
    flag_ref[...] = (needed > dense).astype(jnp.int32)
    slot_ref[...] = (
        jnp.sum(hot_row * offset[:, 0:1].astype(F32), axis=0, keepdims=True).astype(jnp.int32)
        + rank_row
    )

    def combine(pick, block, first):
        for at in range(0, width, piece):
            part = dot(pick, block[:, at : at + piece]).astype(BF16)
            if first:
                out_ref[:, at : at + piece] = part
            else:
                out_ref[:, at : at + piece] += part

    def choose(source, rows):
        fits = offset[pl.ds(source, 1), 0:rows] + iota((1, rows), 1) < capacity
        return ones((iota((tok, rows), 1) + source * most == position[...]) & fits)

    combine(choose(me, most), results.at[me], True)

    def near_back(i, c):
        source = near + lax.rem(place + hn - i, hn)
        back(me, source, False).wait_recv()
        combine(choose(source, most), returned.at[source], False)
        return c

    lax.fori_loop(1, hn, near_back, 0)

    def far_back(i, c):
        source = far + lax.rem(place + hn - i, hn)
        back(me, source, True).wait_recv()
        combine(choose(source, base), returned.at[source, pl.ds(0, base)], False)
        return c

    lax.fori_loop(0, hn, far_back, 0)

    entry = iota((1, dense), 1)
    keep = jnp.zeros((1, dense), jnp.int32)
    for slot in range(hn):
        row = pl.ds(far + slot, 1)
        rank = entry - x_first[row, 0:1]
        inside = (rank >= 0) & (rank < x_size[row, 0:1])
        keep += (inside & (offset[row, 0:1] + rank + base < capacity)).astype(jnp.int32)
    send_back.wait_recv()
    combine(
        ones((iota((tok, dense), 1) == x_position[...]) & (keep > 0)), x_home, False
    )

    send_x.wait_send()
    send_back.wait_send()

    def drain_near(i, c):
        slot = around(i)
        other = near + slot
        go(other, me, False).wait_send()
        back(other, me, False).wait_send()
        forward(other, slot, partner).wait_send()
        gather(other, far + slot, place).wait_send()
        return c

    lax.fori_loop(1, hn, drain_near, 0)

    def drain_far(i, c):
        other = far + i
        go(other, me, True).wait_send()
        back(other, me, True).wait_send()
        return c

    lax.fori_loop(0, hn, drain_far, 0)

    def drain(i, c):
        count(lax.rem(me + i, n), me).wait_send()
        return c

    lax.fori_loop(1, n, drain, 0)

    def drain_dp(i, c):
        total(lax.rem(group + i, dps), group).wait_send()
        return c

    lax.fori_loop(1, dps, drain_dp, 0)


def relayed(tokens, expert_ids, gate_proj, up_proj, down_proj):
    tok, width = tokens.shape
    hidden = gate_proj.shape[2]
    n = lax.axis_size("expert")
    dps = lax.axis_size("dp")
    most = 2 * tok // n
    base = most // 2
    over = most - base
    dense = 5 * most // 4
    capacity = tok * dps
    vmem = pl.BlockSpec(memory_space=pltpu.VMEM)
    anywhere = pl.BlockSpec(memory_space=pltpu.MemorySpace.HBM)
    dma = pltpu.SemaphoreType.DMA
    block = pltpu.VMEM((n, most, width), BF16)
    packed = pltpu.VMEM((dense, width), BF16)
    relay = pltpu.VMEM((n // 2, over, width), BF16)
    table = pltpu.VMEM((n, LANES), jnp.int32)
    column = pltpu.VMEM((tok, 1), jnp.int32)
    mixed, slot, flag = pl.pallas_call(
        functools.partial(relay_kernel, n, dps, most, base, dense, capacity),
        out_shape=(
            jax.ShapeDtypeStruct((tok, width), BF16),
            jax.ShapeDtypeStruct((1, tok), jnp.int32),
            jax.ShapeDtypeStruct((8, LANES), jnp.int32),
        ),
        in_specs=[vmem, vmem, vmem, anywhere, anywhere, anywhere],
        out_specs=(vmem, vmem, vmem),
        scratch_shapes=[
            pltpu.VMEM((width, hidden), BF16),
            pltpu.VMEM((width, hidden), BF16),
            pltpu.VMEM((hidden, width), BF16),
            block, block, block, block,
            packed, packed, packed, packed, relay, relay,
            column, column, table, table, table, table, table,
            table,
            pltpu.VMEM((n, n, LANES), jnp.int32),
            pltpu.VMEM((2, n, LANES), jnp.int32),
            pltpu.VMEM((dps, 2, n, LANES), jnp.int32),
            dma((3,)), dma((n,)), dma((n,)), dma((n,)), dma((n,)),
            dma((n // 2,)), dma((n,)), dma((n,)), dma((n // 2,)), dma((2,)), dma((2,)),
            dma((n,)), dma((n,)), dma((dps,)), dma((dps,)),
        ],
        compiler_params=pltpu.CompilerParams(
            collective_id=0, has_side_effects=True, vmem_limit_bytes=60 * 2**20
        ),
    )(
        expert_ids.reshape(1, tok), expert_ids, tokens, gate_proj, up_proj, down_proj
    )
    return lax.cond(
        flag[0, 0] > 0,
        lambda: padded(tokens, expert_ids, gate_proj, up_proj, down_proj),
        lambda: (mixed, slot.reshape(tok)),
    )


def on_device(tokens, expert_ids, gate_proj, up_proj, down_proj):
    n = lax.axis_size("expert")
    if n == 8 and tokens.shape[0] // n % 16 == 0:
        return relayed(tokens, expert_ids, gate_proj, up_proj, down_proj)
    return direct(tokens, expert_ids, gate_proj, up_proj, down_proj)


def solution(mesh):
    in_specs = (
        P(("dp", "expert"), None),
        P(("dp", "expert"), None),
        P("expert", None, None),
        P("expert", None, None),
        P("expert", None, None),
    )
    out_specs = (P(("dp", "expert"), None), P(("dp", "expert")))
    return jax.shard_map(
        on_device, mesh=mesh, in_specs=in_specs, out_specs=out_specs, check_vma=False
    )
```

profile of v0, /device:TPU:0, one launch (start us, length us, event | category | flops | bytes accessed | tf_op | source)
XLA Modules:
  0.0 170.9 jit_solution(11027792090489377207)
XLA Ops:
  0.6 1.5 copy.11.col_ids
  2.2 0.0 copy-start.1
  2.2 0.0 copy-start.3
  2.2 162.9 %shard_map.70 = (bf16[512,2048]{1,0:T(8,128)(2,1)}, s32[1,512]{1,0:T(1,128)S(1)}, s32[8,128]{1,0:T(8,128)}) custom-call(s32[1,512]{1,0:T(1,128)} %bitcast.47, s32[512,1]{1,0:T(8,128)} %copy.11.col_ids, bf16[512,2048]{1,0:T(8,128)(2,1)} %tok_ref.1, bf16[1,2048,768]{2,1,0:T(8,128)(2,1)} %gate_hbm.1, bf16[1,2048,768]{2,1,0:T(8,128)(2,1)} %up_hbm.1, ...), custom_call_target="tpu_custom_call" | custom-call | tf_op jit(solution)/shard_map/pallas_call | solution.py:806
  165.1 1.2 slice.9
  166.9 0.0 copy-done.1
  166.9 0.0 copy-done.3
  166.9 0.2 conditional.1
  167.2 3.2 %copy.36 = bf16[512,2048]{1,0:T(8,128)(2,1)} copy(bf16[512,2048]{1,0:T(8,128)(2,1)} %get-tuple-element.200) | data formatting | bytes 4194304
  170.3 0.6 copy.37
Async XLA Ops:
  2.2 164.8 %copy-start.1 = (bf16[1,2048,768]{2,1,0:T(8,128)(2,1)S(1)}, bf16[1,2048,768]{2,1,0:T(8,128)(2,1)}, u32[]{:S(2)}) copy-start(bf16[1,2048,768]{2,1,0:T(8,128)(2,1)} %gate_hbm.1) | copy-start | bytes 9437188
  2.2 164.8 %copy-start.3 = (s32[512,1]{0,1:T(1,128)S(1)}, s32[512,1]{0,1:T(1,128)}, u32[]{:S(2)}) copy-start(s32[512,1]{0,1:T(1,128)} %param.12) | copy-start | bytes 6148
where the time goes:
time: 171 us
  Pallas kernels  163 us (95%)
  local copies, waits for them, and re-layouts  6.48 us (4%)
    pallas_call x1, Pallas kernels, relayed(): pl.pallas_call(functools.partial(relay_kernel, n, dps, most, base, dense,...  163 us
    unnamed x7, local copies, waits for them, and re-layouts  5.28 us

commit v1 on v0

v1 whole, which is shorter than its diff:
```python
import functools

import jax
import jax.numpy as jnp
from jax import lax
from jax.experimental import pallas as pl
from jax.experimental.pallas import tpu as pltpu
from jax.sharding import PartitionSpec as P

MESH = pl.DeviceIdType.MESH
F32 = jnp.float32
BF16 = jnp.bfloat16
LANES = 128
NEAR_BLOCKS, FAR_BLOCKS, GO_BLOCKS, DELAY = 18, 19, 13, 3


def spread(step, n):
    half = (step // 2) * (2 * (step % 2) - 1)
    return jnp.where(step == 0, 0, n // 2 + half)


def direct_kernel(
    n, dps, most, capacity,
    row_ids, col_ids, tok_ref, gate_hbm, up_hbm, down_hbm,
    out_ref, slot_ref,
    gate_ref, up_ref, down_ref, outgoing, arrived, results, returned,
    position, offset, counts, count_all, totals, total_all,
    weight_sem, go_send, go_recv, back_send, back_recv,
    count_send, count_recv, total_send, total_recv,
):
    me = lax.axis_index("expert")
    group = lax.axis_index("dp")
    tok = tok_ref.shape[0]
    width = tok_ref.shape[1]

    weights = [
        pltpu.make_async_copy(src.at[0], dst, weight_sem.at[i])
        for i, (src, dst) in enumerate(
            ((gate_hbm, gate_ref), (up_hbm, up_ref), (down_hbm, down_ref))
        )
    ]
    for copy in weights:
        copy.start()

    barrier = pltpu.get_barrier_semaphore()

    def greet(i, c):
        pl.semaphore_signal(
            barrier, inc=1, device_id={"expert": lax.rem(me + i, n)}, device_id_type=MESH
        )
        return c

    def greet_dp(i, c):
        pl.semaphore_signal(
            barrier, inc=1, device_id={"dp": lax.rem(group + i, dps)}, device_id_type=MESH
        )
        return c

    lax.fori_loop(1, n, greet, 0)
    lax.fori_loop(1, dps, greet_dp, 0)

    earlier = lax.broadcasted_iota(jnp.int32, (tok, tok), 0) < lax.broadcasted_iota(
        jnp.int32, (tok, tok), 1
    )
    later = lax.broadcasted_iota(jnp.int32, (tok, tok), 0) > lax.broadcasted_iota(
        jnp.int32, (tok, tok), 1
    )
    ids_row = row_ids[...]
    hot_row = (ids_row == lax.broadcasted_iota(jnp.int32, (n, tok), 0)).astype(F32)
    before_row = jnp.dot(
        hot_row.astype(BF16), earlier.astype(F32).astype(BF16), preferred_element_type=F32
    )
    rank_row = jnp.sum(before_row * hot_row, axis=0, keepdims=True).astype(jnp.int32)
    pos_row = ids_row * most + rank_row
    counts[...] = jnp.broadcast_to(
        jnp.sum(hot_row, axis=1, keepdims=True), (n, LANES)
    ).astype(jnp.int32)

    ids_col = col_ids[...]
    hot_col = (ids_col == lax.broadcasted_iota(jnp.int32, (tok, n), 1)).astype(F32)
    before_col = jnp.dot(
        later.astype(F32).astype(BF16), hot_col.astype(BF16), preferred_element_type=F32
    )
    rank_col = jnp.sum(before_col * hot_col, axis=1, keepdims=True).astype(jnp.int32)
    position[...] = ids_col * most + rank_col

    def go(dest, source):
        return pltpu.make_async_remote_copy(
            src_ref=outgoing.at[dest], dst_ref=arrived.at[source],
            send_sem=go_send.at[dest], recv_sem=go_recv.at[source],
            device_id={"expert": dest}, device_id_type=MESH,
        )

    def back(dest, source):
        return pltpu.make_async_remote_copy(
            src_ref=results.at[dest], dst_ref=returned.at[source],
            send_sem=back_send.at[dest], recv_sem=back_recv.at[source],
            device_id={"expert": dest}, device_id_type=MESH,
        )

    def count(dest, source):
        return pltpu.make_async_remote_copy(
            src_ref=counts, dst_ref=count_all.at[source],
            send_sem=count_send.at[dest], recv_sem=count_recv.at[source],
            device_id={"expert": dest}, device_id_type=MESH,
        )

    def total(dest, source):
        return pltpu.make_async_remote_copy(
            src_ref=totals, dst_ref=total_all.at[source],
            send_sem=total_send.at[dest], recv_sem=total_recv.at[source],
            device_id={"dp": dest}, device_id_type=MESH,
        )

    def pack(dest):
        pick = (
            lax.broadcasted_iota(jnp.int32, (most, tok), 0) + dest * most == pos_row
        ).astype(F32).astype(BF16)
        return jnp.dot(pick, tok_ref[...], preferred_element_type=F32).astype(BF16)

    pl.semaphore_wait(barrier, n + dps - 2)

    def dispatch(i, c):
        dest = lax.rem(me + spread(i, n), n)
        outgoing[dest] = pack(dest)
        go(dest, me).start()
        return c

    lax.fori_loop(1, n, dispatch, 0)

    def tell(i, c):
        count(lax.rem(me + i, n), me).start()
        return c

    lax.fori_loop(1, n, tell, 0)
    count_all[me] = counts[...]
    arrived[me] = pack(me)

    for copy in weights:
        copy.wait()

    def ffn(source):
        rows = arrived[source]
        gate = jnp.dot(rows, gate_ref[...], preferred_element_type=F32)
        up = jnp.dot(rows, up_ref[...], preferred_element_type=F32)
        hidden = (gate / (1.0 + jnp.exp(-gate)) * up).astype(BF16)
        return jnp.dot(hidden, down_ref[...], preferred_element_type=F32).astype(BF16)

    def expert_step(i, c):
        source = lax.rem(me + n - spread(i, n), n)

        @pl.when(i > 0)
        def _():
            go(me, source).wait_recv()

        results[source] = ffn(source)

        @pl.when(i > 0)
        def _():
            back(source, me).start()

        return c

    lax.fori_loop(0, n, expert_step, 0)

    def heard(i, c):
        count(me, lax.rem(me + i, n)).wait_recv()
        return c

    lax.fori_loop(1, n, heard, 0)

    def add(i, carry):
        inner, whole = carry
        here = count_all[i]
        return inner + here * (i < me).astype(jnp.int32), whole + here

    zero = jnp.zeros((n, LANES), jnp.int32)
    inner, whole = lax.fori_loop(0, n, add, (zero, zero))
    totals[...] = whole

    def tell_dp(i, c):
        total(lax.rem(group + i, dps), group).start()
        return c

    lax.fori_loop(1, dps, tell_dp, 0)
    total_all[group] = whole

    def heard_dp(i, c):
        total(group, lax.rem(group + i, dps)).wait_recv()
        return c

    lax.fori_loop(1, dps, heard_dp, 0)

    def add_dp(i, outer):
        return outer + total_all[i] * (i < group).astype(jnp.int32)

    offset[...] = inner + lax.fori_loop(0, dps, add_dp, zero)
    slot_ref[...] = (
        jnp.sum(
            hot_row * offset[:, 0:1].astype(F32), axis=0, keepdims=True
        ).astype(jnp.int32)
        + rank_row
    )

    piece = min(width, 512)

    def combine(source, block, first):
        lane = lax.broadcasted_iota(jnp.int32, (tok, most), 1)
        fits = offset[pl.ds(source, 1), 0:most] + lax.broadcasted_iota(
            jnp.int32, (1, most), 1
        ) < capacity
        pick = (lane + source * most == position[...]) & fits
        pick = pick.astype(F32).astype(BF16)
        for at in range(0, width, piece):
            part = jnp.dot(
                pick, block[source, :, at : at + piece], preferred_element_type=F32
            ).astype(BF16)
            if first:
                out_ref[:, at : at + piece] = part
            else:
                out_ref[:, at : at + piece] += part

    combine(me, results, True)

    def combine_step(i, c):
        source = lax.rem(me + n - spread(i, n), n)
        back(me, source).wait_recv()
        combine(source, returned, False)
        return c

    lax.fori_loop(1, n, combine_step, 0)

    def drain(i, c):
        other = lax.rem(me + i, n)
        go(other, me).wait_send()
        back(other, me).wait_send()
        count(other, me).wait_send()
        return c

    lax.fori_loop(1, n, drain, 0)

    def drain_dp(i, c):
        total(lax.rem(group + i, dps), group).wait_send()
        return c

    lax.fori_loop(1, dps, drain_dp, 0)


def direct(tokens, expert_ids, gate_proj, up_proj, down_proj):
    tok, width = tokens.shape
    hidden = gate_proj.shape[2]
    n = lax.axis_size("expert")
    dps = lax.axis_size("dp")
    most = 2 * tok // n
    capacity = tok * dps
    vmem = pl.BlockSpec(memory_space=pltpu.VMEM)
    anywhere = pl.BlockSpec(memory_space=pltpu.MemorySpace.HBM)
    dma = pltpu.SemaphoreType.DMA
    block = pltpu.VMEM((n, most, width), BF16)
    mixed, slot = pl.pallas_call(
        functools.partial(direct_kernel, n, dps, most, capacity),
        out_shape=(
            jax.ShapeDtypeStruct((tok, width), BF16),
            jax.ShapeDtypeStruct((1, tok), jnp.int32),
        ),
        in_specs=[vmem, vmem, vmem, anywhere, anywhere, anywhere],
        out_specs=(vmem, vmem),
        scratch_shapes=[
            pltpu.VMEM((width, hidden), BF16),
            pltpu.VMEM((width, hidden), BF16),
            pltpu.VMEM((hidden, width), BF16),
            block, block, block, block,
            pltpu.VMEM((tok, 1), jnp.int32),
            pltpu.VMEM((n, LANES), jnp.int32),
            pltpu.VMEM((n, LANES), jnp.int32),
            pltpu.VMEM((n, n, LANES), jnp.int32),
            pltpu.VMEM((n, LANES), jnp.int32),
            pltpu.VMEM((dps, n, LANES), jnp.int32),
            dma((3,)), dma((n,)), dma((n,)), dma((n,)), dma((n,)),
            dma((n,)), dma((n,)), dma((dps,)), dma((dps,)),
        ],
        compiler_params=pltpu.CompilerParams(
            collective_id=0, has_side_effects=True, vmem_limit_bytes=60 * 2**20
        ),
    )(
        expert_ids.reshape(1, tok), expert_ids, tokens, gate_proj, up_proj, down_proj
    )
    return mixed, slot.reshape(tok)


def entering(part, axis, combine, identity):
    place = lax.axis_index(axis)
    gathered = lax.all_gather(part, axis)
    state = jnp.zeros_like(part) + jnp.asarray(identity, part.dtype)

    def one(hop, state):
        return combine(state, lax.dynamic_index_in_dim(gathered, hop, 0, False))

    return lax.fori_loop(0, place, one, state)


def add_counts(earlier, later):
    return earlier + later


def expert_ffn(rows, gate_proj, up_proj, down_proj):
    gate_val = jnp.dot(rows, gate_proj[0], preferred_element_type=jnp.float32)
    up_val = jnp.dot(rows, up_proj[0], preferred_element_type=jnp.float32)
    hidden = (jax.nn.silu(gate_val) * up_val).astype(jnp.bfloat16)
    return jnp.dot(hidden, down_proj[0], preferred_element_type=jnp.float32).astype(jnp.bfloat16)


def padded(tokens, expert_ids, gate_proj, up_proj, down_proj):
    tok_rows, width = tokens.shape
    experts_all = lax.axis_size("expert")
    most = 2 * tok_rows // experts_all
    capacity = tok_rows * lax.axis_size("dp")
    choices = expert_ids[:, 0]
    onehot = (choices[:, None] == jnp.arange(experts_all, dtype=jnp.int32)[None, :]).astype(
        jnp.int32
    )
    counts = jnp.sum(onehot, axis=0)
    inner = entering(counts, "expert", add_counts, jnp.zeros_like(counts))
    totals = lax.psum(counts, "expert")
    outer = entering(totals, "dp", add_counts, jnp.zeros_like(totals))
    offset = inner + outer
    before = jnp.cumsum(onehot, axis=0) - onehot
    local_rank = jnp.sum(before * onehot, axis=1)
    global_slot = (jnp.sum(onehot * offset[None, :], axis=1) + local_rank).astype(jnp.int32)
    is_kept = global_slot < capacity
    position = choices * most + local_rank
    targets = jnp.arange(experts_all * most, dtype=jnp.int32)
    dispatch = ((targets[:, None] == position[None, :]) & is_kept[None, :]).astype(jnp.bfloat16)
    outgoing = jnp.dot(dispatch, tokens, preferred_element_type=jnp.float32).astype(jnp.bfloat16)
    outgoing = outgoing.reshape(experts_all, most, width)
    arrived = lax.all_to_all(outgoing, "expert", split_axis=0, concat_axis=0, tiled=True)
    sources, slots_here, _ = arrived.shape
    flat = arrived.reshape(sources * slots_here, width)
    returned = lax.all_to_all(
        expert_ffn(flat, gate_proj, up_proj, down_proj).reshape(sources, slots_here, width),
        "expert",
        split_axis=0,
        concat_axis=0,
        tiled=True,
    )
    flat_back = returned.reshape(experts_all * most, width)
    mixed = lax.dot_general(
        dispatch, flat_back, (((0,), (0,)), ((), ())), preferred_element_type=jnp.float32
    )
    return (mixed.astype(jnp.bfloat16), global_slot)


NEAR_ORDER = {
    "A": (("go", "o", "p"), ("go", "o", "q"), ("go", "o", "i"),
          ("ret", "o", "i"), ("ret", "o", "p"), ("ret", "o", "q")),
    "M": (("go", "i", "p"), ("go", "i", "q"), ("go", "o", "p"), ("go", "o", "q"),
          ("ret", "i", "p"), ("ret", "i", "q"), ("ret", "o", "p"), ("ret", "o", "q")),
    "B": (("go", "i", "o"), ("go", "p", "o"), ("go", "q", "o"),
          ("ret", "i", "o"), ("ret", "p", "o"), ("ret", "q", "o")),
}
FLIP = {"o": "q", "i": "p", "p": "i", "q": "o"}
FAR_KEY = 4096
LOCAL_KEY = 8192


def lay_streams(rows_of, block, delay):
    place, end = {}, {}
    queue = {(s, h): list(NEAR_ORDER[s]) for s in "AMB" for h in (0, 1)}
    zero = jnp.zeros((1, LANES), jnp.int32)
    for name in queue:
        end[name] = zero
    while any(queue.values()):
        for (s, h), runs in queue.items():
            while runs:
                kind, a, b = runs[0]
                fa, fb = FLIP[a], FLIP[b]
                need = None
                if s == "A" and kind == "ret":
                    need = (("B", h, "go", b, a), 3 + delay)
                elif s == "M" and a == "o":
                    need = (("A", h, kind, a, b), 2)
                elif s == "M" and kind == "ret":
                    need = (("M", 1 - h, "go", fb, fa), 3)
                elif s == "B" and a != "i":
                    need = (("M", 1 - h, kind, fa, fb), 2 - delay)
                elif s == "B" and kind == "ret":
                    need = (("A", h, "go", b, a), 3 - delay)
                if need is not None and need[0] not in place:
                    break
                size = rows_of(h, a, b) if kind == "go" else rows_of(h, b, a)
                first = end[(s, h)]
                if need is not None:
                    ready = place[need[0]][0] + block * need[1]
                    first = jnp.where(size > 0, jnp.maximum(first, ready), first)
                place[(s, h, kind, a, b)] = (first, size)
                end[(s, h)] = first + size
                runs.pop(0)
    return place, end


def stream_kernel(
    n, dps, capacity, block, near_blocks, far_blocks, go_blocks, delay,
    row_ids, tok_hbm, gate_hbm, up_hbm, down_hbm,
    out_ref, slot_ref, flag_ref,
    gate_ref, up_ref, down_ref, pool, inbox, outbox,
    tok_key, in_key, position, counts, count_all, totals, total_all,
    tok_sem, own_sem, pair_send, pair_recv, near_send, near_recv, far_send, far_recv,
    count_send, count_recv, total_send, total_recv,
):
    me = lax.axis_index("expert")
    group = lax.axis_index("dp")
    tok = row_ids.shape[1]
    width = pool.shape[1]
    hidden = gate_ref.shape[2]
    core = lax.rem(me, 2)
    chip = lax.div(me, 2)
    half = lax.div(chip, 2)
    roles = {"o": 3 * half, "i": 1 + half, "p": 2 - half, "q": 3 - 3 * half}
    inner = chip == roles["i"]
    is_inner = inner.astype(jnp.int32)
    is_outer = 1 - is_inner
    near_dev = me + 2 - 4 * lax.rem(chip, 2)
    far_dev = 2 * (3 - chip) + core
    pair_dev = me + 1 - 2 * core
    two = 2 * block
    blocks = inbox.shape[0] // two
    steps = max(far_blocks, near_blocks + delay)
    local_at = tok + blocks * two
    piece = min(width, 512)
    ring = outbox.shape[0]

    def iota(shape, axis):
        return lax.broadcasted_iota(jnp.int32, shape, axis)

    def ones(mask):
        return mask.astype(F32).astype(BF16)

    def dot(a, b):
        return jnp.dot(a, b, preferred_element_type=F32)

    load_tok = pltpu.make_async_copy(tok_hbm, pool.at[pl.ds(0, tok)], tok_sem.at[0])
    load_tok.start()
    mine_down = pl.ds(pl.multiple_of(core * hidden, hidden), hidden)
    pairs = (
        (gate_hbm, gate_ref.at[core]), (up_hbm, up_ref.at[core]),
        (down_hbm, down_ref.at[mine_down]),
    )
    own = [
        pltpu.make_async_copy(src.at[0], dst, own_sem.at[i])
        for i, (src, dst) in enumerate(pairs)
    ]
    share = [
        pltpu.make_async_remote_copy(
            src_ref=src.at[0], dst_ref=dst, send_sem=pair_send.at[i],
            recv_sem=pair_recv.at[i], device_id={"expert": pair_dev}, device_id_type=MESH,
        )
        for i, (src, dst) in enumerate(pairs)
    ]
    other_down = pl.ds(pl.multiple_of((1 - core) * hidden, hidden), hidden)
    arriving = [
        pltpu.make_async_remote_copy(
            src_ref=src.at[0], dst_ref=dst, send_sem=pair_send.at[i],
            recv_sem=pair_recv.at[i], device_id={"expert": pair_dev}, device_id_type=MESH,
        )
        for i, (src, dst) in enumerate((
            (gate_hbm, gate_ref.at[1 - core]), (up_hbm, up_ref.at[1 - core]),
            (down_hbm, down_ref.at[other_down]),
        ))
    ]
    for copy in own:
        copy.start()

    barrier = pltpu.get_barrier_semaphore()

    def greet(i, c):
        pl.semaphore_signal(
            barrier, inc=1, device_id={"expert": lax.rem(me + i, n)}, device_id_type=MESH
        )
        return c

    def greet_dp(i, c):
        pl.semaphore_signal(
            barrier, inc=1, device_id={"dp": lax.rem(group + i, dps)}, device_id_type=MESH
        )
        return c

    lax.fori_loop(1, n, greet, 0)
    lax.fori_loop(1, dps, greet_dp, 0)

    ids_row = row_ids[...]
    hot_row = (ids_row == iota((n, tok), 0)).astype(F32)
    before_row = dot(hot_row.astype(BF16), ones(iota((tok, tok), 0) < iota((tok, tok), 1)))
    rank_row = jnp.sum(before_row * hot_row, axis=0, keepdims=True).astype(jnp.int32)
    mine = jnp.broadcast_to(jnp.sum(hot_row, axis=1, keepdims=True), (n, LANES))
    counts[...] = mine.astype(jnp.int32)
    row8 = iota((n, n), 0)
    shift = ones((iota((n, n), 1) + 1 == row8) & (lax.rem(row8, 2) == 1))
    skip = dot(shift, mine.astype(BF16))
    pair_rank = rank_row + jnp.sum(
        hot_row * skip[:, 0:1], axis=0, keepdims=True
    ).astype(jnp.int32)
    pair_row = lax.shift_right_logical(ids_row, 1)

    def own_rows(role):
        e = 2 * roles[role]
        return (counts[pl.ds(e, 1), :] + counts[pl.ds(e + 1, 1), :])[:, 0:1]

    zero1 = jnp.zeros((1, 1), jnp.int32)
    to_o = jnp.where(inner, zero1, LOCAL_KEY)
    to_i = jnp.where(inner, LOCAL_KEY, own_rows("p") + own_rows("q"))
    to_p = jnp.where(inner, zero1 + FAR_KEY, 0)
    to_q = own_rows("p") + jnp.where(inner, FAR_KEY, 0)
    key = jnp.zeros((1, tok), jnp.int32)
    for role, base in (("o", to_o), ("i", to_i), ("p", to_p), ("q", to_q)):
        key = jnp.where(pair_row == roles[role], base + pair_rank, key)
    tok_key[...] = key

    def near_copy(j, slot):
        return pltpu.make_async_remote_copy(
            src_ref=outbox.at[slot, pl.ds(0, block)],
            dst_ref=inbox.at[pl.ds(pl.multiple_of(j * two, two), block)],
            send_sem=near_send.at[slot], recv_sem=near_recv.at[j],
            device_id={"expert": near_dev}, device_id_type=MESH,
        )

    def far_copy(j, slot):
        return pltpu.make_async_remote_copy(
            src_ref=outbox.at[slot, pl.ds(block, block)],
            dst_ref=inbox.at[pl.ds(pl.multiple_of(j * two + block, block), block)],
            send_sem=far_send.at[slot], recv_sem=far_recv.at[j],
            device_id={"expert": far_dev}, device_id_type=MESH,
        )

    def count(dest, source):
        return pltpu.make_async_remote_copy(
            src_ref=counts, dst_ref=count_all.at[source],
            send_sem=count_send.at[dest], recv_sem=count_recv.at[source],
            device_id={"expert": dest}, device_id_type=MESH,
        )

    def total(dest, source):
        return pltpu.make_async_remote_copy(
            src_ref=totals, dst_ref=total_all.at[source],
            send_sem=total_send.at[dest], recv_sem=total_recv.at[source],
            device_id={"dp": dest}, device_id_type=MESH,
        )

    def sent(k):
        slot = lax.rem(k, ring)
        near_at = k - delay * is_inner

        @pl.when((near_at >= 0) & (near_at < near_blocks))
        def _():
            near_copy(near_at, slot).wait_send()

        @pl.when(inner & (k < far_blocks))
        def _():
            far_copy(k, slot).wait_send()

    def send(k, low, high):
        slot = lax.rem(k, ring)
        near_at = k - delay * is_inner

        @pl.when(k >= ring)
        def _():
            sent(k - ring)

        @pl.when(inner | (k < near_blocks))
        def _():
            row = iota((two, 1), 0)
            want = jnp.where(
                row < block, near_at * block + row, FAR_KEY + k * block + row - block
            )
            picks = []
            if low < tok:
                picks.append(ones(want == tok_key[...]))
            if high > tok:
                picks.append(ones(want == in_key[:, max(low, tok) - tok : high - tok]))
            pick = picks[0] if len(picks) == 1 else jnp.concatenate(picks, axis=1)
            for at in range(0, width, piece):
                outbox[slot, :, at : at + piece] = dot(
                    pick, pool[low:high, at : at + piece]
                ).astype(BF16)

        @pl.when((near_at >= 0) & (near_at < near_blocks))
        def _():
            near_copy(near_at, slot).start()

        @pl.when(inner & (k < far_blocks))
        def _():
            far_copy(k, slot).start()

    def arrive(b):
        at = pl.multiple_of(b * two, two)

        @pl.when((b >= 0) & (b < near_blocks))
        def _():
            near_copy(b, 0).wait_recv()
            pool[pl.ds(tok + at, block), :] = inbox[pl.ds(at, block), :]

        @pl.when(inner & (b >= 0) & (b < far_blocks))
        def _():
            far_copy(b, 0).wait_recv()
            pool[pl.ds(tok + at + block, block), :] = inbox[pl.ds(at + block, block), :]

    def ffn(rows, code):
        parts = []
        wide = jnp.broadcast_to(code, (two, hidden))
        for parity in (0, 1):
            gate = dot(rows, gate_ref[parity])
            up = dot(rows, up_ref[parity])
            act = gate / (1.0 + jnp.exp(-gate)) * up
            parts.append(jnp.where(wide == parity + 1, act, 0.0).astype(BF16))
        act = jnp.concatenate(parts, axis=1)
        return [
            dot(act, down_ref[:, at : at + piece]) for at in range(0, width, piece)
        ]

    spare = pool.at[pl.ds(tok, blocks * two)]

    def clear(i, c):
        spare[pl.ds(pl.multiple_of(i * two, two), two), :] = jnp.zeros((two, width), BF16)
        return c

    lax.fori_loop(0, blocks, clear, 0)
    load_tok.wait()
    pl.semaphore_wait(barrier, n + dps - 2)

    def tell(i, c):
        count(lax.rem(me + i, n), me).start()
        return c

    lax.fori_loop(1, n, tell, 0)
    count_all[me] = counts[...]

    def first_steps(k, c):
        send(k, 0, tok)
        return c

    lax.fori_loop(0, 2, first_steps, 0)
    for copy in share:
        copy.start()

    def heard(i, c):
        count(me, lax.rem(me + i, n)).wait_recv()
        return c

    lax.fori_loop(1, n, heard, 0)

    def rows_of(lane):
        def get(h, a, b):
            a, b = (FLIP[a], FLIP[b]) if h else (a, b)
            dev, e = 2 * roles[a] + lane, 2 * roles[b]
            return count_all[dev, pl.ds(e, 1), :] + count_all[dev, pl.ds(e + 1, 1), :]

        return get

    def even(a):
        return count_all[2 * roles[a] + core, pl.ds(2 * chip, 1), :][:, 0:1]

    place, ends = lay_streams(rows_of(core), block, delay)
    over = jnp.zeros((1, LANES), jnp.int32)
    for lane_place, lane_ends in (
        (place, ends), lay_streams(rows_of(1 - core), block, delay)
    ):
        for (s, _), end in lane_ends.items():
            limit = (far_blocks if s == "M" else near_blocks) * block
            over = jnp.maximum(over, (end > limit).astype(jnp.int32))
        for name, (first, size) in lane_place.items():
            if name[2] == "go":
                late = (first + size > go_blocks * block) & (size > 0)
                over = jnp.maximum(over, late.astype(jnp.int32))

    def at(name):
        first, size = place[name]
        return first[:, 0:1], size[:, 0:1]

    def choose(a, b):
        return tuple(jnp.where(inner, x, y) for x, y in zip(at(a), at(b)))

    def start(name):
        return at(name)[0]

    lane = iota((1, blocks * two), 1)
    inside = lax.rem(lane, two)
    is_far = inside >= block
    spot = lax.div(lane, two) * block + lax.rem(inside, block)
    nowhere = zero1 - 65536
    code = jnp.full((1, blocks * two), -1, jnp.int32)
    near_runs = (
        (("A", 0, "go", "o", "p"), ("B", 0, "go", "i", "o"),
         FAR_KEY + start(("M", 0, "go", "o", "p")), start(("A", 0, "ret", "o", "i"))),
        (("A", 0, "go", "o", "q"), ("B", 0, "go", "p", "o"),
         FAR_KEY + start(("M", 0, "go", "o", "q")), start(("A", 0, "ret", "o", "p"))),
        (("A", 0, "go", "o", "i"), ("B", 0, "go", "q", "o"),
         start(("B", 0, "ret", "i", "o")), start(("A", 0, "ret", "o", "q"))),
        (("A", 0, "ret", "o", "p"), ("B", 0, "ret", "p", "o"),
         FAR_KEY + start(("M", 0, "ret", "o", "p")), nowhere),
        (("A", 0, "ret", "o", "q"), ("B", 0, "ret", "q", "o"),
         FAR_KEY + start(("M", 0, "ret", "o", "q")), nowhere),
    )
    for in_run, out_run, to_in, to_out in near_runs:
        first, size = choose(in_run, out_run)
        to = jnp.where(inner, to_in, to_out)
        hit = (spot >= first) & (spot < first + size) & jnp.logical_not(is_far)
        code = jnp.where(hit, spot + (to - first), code)
    far_runs = (
        (("M", 1, "go", "i", "p"), FAR_KEY + start(("M", 0, "ret", "i", "p"))),
        (("M", 1, "go", "i", "q"), start(("B", 0, "go", "p", "o"))),
        (("M", 1, "go", "o", "p"), FAR_KEY + start(("M", 0, "ret", "i", "q"))),
        (("M", 1, "go", "o", "q"), start(("B", 0, "go", "q", "o"))),
        (("M", 1, "ret", "i", "q"), start(("B", 0, "ret", "p", "o"))),
        (("M", 1, "ret", "o", "q"), start(("B", 0, "ret", "q", "o"))),
    )
    for run, to in far_runs:
        first, size = at(run)
        hit = (spot >= first) & (spot < first + size) & is_far
        code = jnp.where(hit, spot + (to - first), code)
    in_key[...] = code

    mine_runs = []
    for in_run, out_run, far_side, a_in, a_out in (
        (("A", 0, "go", "o", "i"), ("B", 0, "go", "i", "o"), 0, "o", "i"),
        (("M", 1, "go", "i", "p"), ("B", 0, "go", "p", "o"), 1, "p", "p"),
        (("M", 1, "go", "o", "p"), ("B", 0, "go", "q", "o"), 1, "q", "q"),
    ):
        first, size = choose(in_run, out_run)
        split = jnp.where(inner, even(a_in), even(a_out))
        mine_runs.append((first, size, split, far_side * is_inner))

    def mark(b):
        row = iota((two, 1), 0)
        side = lax.div(row, block)
        spot = b * block + lax.rem(row, block)
        code = jnp.zeros((two, 1), jnp.int32)
        for first, size, split, which in mine_runs:
            hit = (spot >= first) & (spot < first + size) & (side == which)
            code = jnp.where(hit, jnp.where(spot - first >= split, 2, 1), code)
        return code

    home = zero1 + local_at

    def pool_at(run, side):
        def get(rank):
            spot = start(run) + rank
            return (
                tok + lax.div(spot, block) * two + lax.rem(spot, block) + side * block
            )

        return get

    back_in = {
        "o": pool_at(("A", 0, "ret", "o", "i"), 0),
        "p": pool_at(("M", 1, "ret", "i", "p"), 1),
        "q": pool_at(("M", 1, "ret", "o", "p"), 1),
        "i": lambda rank: home + rank,
    }
    back_out = {
        "i": pool_at(("B", 0, "ret", "i", "o"), 0),
        "p": pool_at(("B", 0, "ret", "p", "o"), 0),
        "q": pool_at(("B", 0, "ret", "q", "o"), 0),
        "o": lambda rank: home + rank,
    }
    from_row = jnp.zeros((1, tok), jnp.int32)
    for role in "oipq":
        found = jnp.where(inner, back_in[role](pair_rank), back_out[role](pair_rank))
        from_row = jnp.where(pair_row == roles[role], found, from_row)

    def add(i, carry):
        before, whole = carry
        here = count_all[i]
        return before + here * (i < me).astype(jnp.int32), whole + here

    zero = jnp.zeros((n, LANES), jnp.int32)
    before, whole = lax.fori_loop(0, n, add, (zero, zero))
    over = jnp.broadcast_to(over, (n, LANES))
    totals[0] = whole
    totals[1] = over
    total_all[group, 0] = whole
    total_all[group, 1] = over

    def tell_dp(i, c):
        total(lax.rem(group + i, dps), group).start()
        return c

    lax.fori_loop(1, dps, tell_dp, 0)

    def work(b):
        at = pl.multiple_of(tok + b * two, two)
        code = mark(b)
        done = ffn(pool[pl.ds(at, two), :], code)
        wide = jnp.broadcast_to(code, (two, piece))
        for i, part in enumerate(done):
            cols = slice(i * piece, (i + 1) * piece)
            raw = pool[pl.ds(at, two), cols].astype(F32)
            pool[pl.ds(at, two), cols] = jnp.where(wide > 0, part, raw).astype(BF16)

    def step(low, high, busy):
        def run(k, c):
            b = k - 2 - delay * is_outer
            arrive(b)
            send(k, low, high)
            if busy:
                @pl.when((b >= 0) & (b < go_blocks))
                def _():
                    work(b)

            return c

        return run

    def local(i, c):
        rank = i * two + iota((two, 1), 0)
        rows = dot(ones(rank + LOCAL_KEY == tok_key[...]), pool[0:tok, :]).astype(BF16)
        e = 2 * chip
        first = counts[pl.ds(e, 1), :][:, 0:1]
        both = first + counts[pl.ds(e + 1, 1), :][:, 0:1]
        code = jnp.where(rank < both, jnp.where(rank >= first, 2, 1), 0)
        at = pl.multiple_of(local_at + i * two, two)
        for j, part in enumerate(ffn(rows, code)):
            pool[pl.ds(at, two), j * piece : (j + 1) * piece] = part.astype(BF16)
        return c

    cut = tok // block
    last = go_blocks + 2 + delay
    lax.fori_loop(2, 3, step(0, tok + two, False), 0)
    for copy in own:
        copy.wait()
    for copy in arriving:
        copy.wait_recv()

    @pl.when(inner)
    def _():
        work(0)

    lax.fori_loop(3, cut, step(0, tok + (cut - 2) * two, True), 0)
    lax.fori_loop(cut, last, step(tok, tok + (last - 2) * two, True), 0)
    lax.fori_loop(last, steps, step(tok, local_at, False), 0)
    lax.fori_loop(0, 2, local, 0)

    def heard_dp(i, c):
        total(group, lax.rem(group + i, dps)).wait_recv()
        return c

    lax.fori_loop(1, dps, heard_dp, 0)

    def add_dp(i, carry):
        outer, most = carry
        return (
            outer + total_all[i, 0] * (i < group).astype(jnp.int32),
            jnp.maximum(most, total_all[i, 1]),
        )

    outer, most = lax.fori_loop(0, dps, add_dp, (zero, over))
    offset = before + outer
    flag_ref[...] = most
    slot = jnp.sum(
        hot_row * offset[:, 0:1].astype(F32), axis=0, keepdims=True
    ).astype(jnp.int32) + rank_row
    slot_ref[...] = slot
    from_row = jnp.where(slot < capacity, from_row, 0)
    position[...] = jnp.transpose(
        jnp.broadcast_to(from_row, (8, tok)).astype(F32)
    )[:, 0:1].astype(jnp.int32)

    span = 4 * two

    def combine(at, size, first):
        pick = ones(position[...] == iota((1, size), 1) + at)
        rows = pl.ds(at if isinstance(at, int) else pl.multiple_of(at, two), size)
        for col in range(0, width, piece):
            part = dot(pick, pool[rows, col : col + piece]).astype(BF16)
            if first:
                out_ref[:, col : col + piece] = part
            else:
                out_ref[:, col : col + piece] += part

    seen = (steps - 2 - delay) * two // span
    combine(tok, span, True)

    def combine_step(c, carry):
        combine(tok + c * span, span, False)
        return carry

    lax.fori_loop(1, seen, combine_step, 0)

    def late(b, c):
        arrive(b)
        return c

    lax.fori_loop(steps - 2 - delay * is_outer, near_blocks, late, 0)
    rest = tok + seen * span
    combine(rest, pool.shape[0] - rest, False)

    def flush(k, c):
        sent(k)
        return c

    lax.fori_loop(steps - ring, steps, flush, 0)
    for copy in share:
        copy.wait_send()

    def drain(i, c):
        count(lax.rem(me + i, n), me).wait_send()
        return c

    lax.fori_loop(1, n, drain, 0)

    def drain_dp(i, c):
        total(lax.rem(group + i, dps), group).wait_send()
        return c

    lax.fori_loop(1, dps, drain_dp, 0)


def streamed(tokens, expert_ids, gate_proj, up_proj, down_proj):
    tok, width = tokens.shape
    hidden = gate_proj.shape[2]
    n = lax.axis_size("expert")
    dps = lax.axis_size("dp")
    capacity = tok * dps
    block = tok // n
    near_blocks, far_blocks, go_blocks, delay = NEAR_BLOCKS, FAR_BLOCKS, GO_BLOCKS, DELAY
    blocks = max(near_blocks, far_blocks)
    ring = 4
    vmem = pl.BlockSpec(memory_space=pltpu.VMEM)
    anywhere = pl.BlockSpec(memory_space=pltpu.MemorySpace.HBM)
    dma = pltpu.SemaphoreType.DMA
    table = pltpu.VMEM((n, LANES), jnp.int32)
    mixed, slot, flag = pl.pallas_call(
        functools.partial(
            stream_kernel, n, dps, capacity, block, near_blocks, far_blocks, go_blocks, delay
        ),
        out_shape=(
            jax.ShapeDtypeStruct((tok, width), BF16),
            jax.ShapeDtypeStruct((1, tok), jnp.int32),
            jax.ShapeDtypeStruct((n, LANES), jnp.int32),
        ),
        in_specs=[vmem, anywhere, anywhere, anywhere, anywhere],
        out_specs=(vmem, vmem, vmem),
        scratch_shapes=[
            pltpu.VMEM((2, width, hidden), BF16),
            pltpu.VMEM((2, width, hidden), BF16),
            pltpu.VMEM((2 * hidden, width), BF16),
            pltpu.VMEM((tok + 2 * block * blocks + 4 * block, width), BF16),
            pltpu.VMEM((2 * block * blocks, width), BF16),
            pltpu.VMEM((ring, 2 * block, width), BF16),
            pltpu.VMEM((1, tok), jnp.int32),
            pltpu.VMEM((1, 2 * block * blocks), jnp.int32),
            pltpu.VMEM((tok, 1), jnp.int32),
            table,
            pltpu.VMEM((n, n, LANES), jnp.int32),
            pltpu.VMEM((2, n, LANES), jnp.int32),
            pltpu.VMEM((dps, 2, n, LANES), jnp.int32),
            dma((1,)), dma((3,)), dma((3,)), dma((3,)),
            dma((ring,)), dma((near_blocks,)), dma((ring,)), dma((far_blocks,)),
            dma((n,)), dma((n,)), dma((dps,)), dma((dps,)),
        ],
        compiler_params=pltpu.CompilerParams(
            collective_id=0, has_side_effects=True, vmem_limit_bytes=60 * 2**20
        ),
    )(expert_ids.reshape(1, tok), tokens, gate_proj, up_proj, down_proj)
    return lax.cond(
        flag[0, 0] > 0,
        lambda: padded(tokens, expert_ids, gate_proj, up_proj, down_proj),
        lambda: (mixed, slot.reshape(tok)),
    )


def on_device(tokens, expert_ids, gate_proj, up_proj, down_proj):
    n = lax.axis_size("expert")
    if n == 8 and tokens.shape[0] // n % 64 == 0:
        return streamed(tokens, expert_ids, gate_proj, up_proj, down_proj)
    return direct(tokens, expert_ids, gate_proj, up_proj, down_proj)


def solution(mesh):
    in_specs = (
        P(("dp", "expert"), None),
        P(("dp", "expert"), None),
        P("expert", None, None),
        P("expert", None, None),
        P("expert", None, None),
    )
    out_specs = (P(("dp", "expert"), None), P(("dp", "expert")))
    return jax.shard_map(
        on_device, mesh=mesh, in_specs=in_specs, out_specs=out_specs, check_vma=False
    )
```

time: 171 us -> 140 us (0.82)
  Pallas kernels: 163 us -> 133 us
    pallas_call x1, Pallas kernels: 163 us -> 133 us  [streamed(): pl.pallas_call(functools.partial(stream_kernel, n, dps, capacity, block,...]
    unnamed x7 -> x6, local copies, waits for them, and re-layouts: 5.28 us -> 3.75 us
where the time goes in v1:
time: 140 us; the launch traced here: 139 us
  Pallas kernels  133 us (95%)
  local copies, waits for them, and re-layouts  4.94 us (4%)
    pallas_call x1, Pallas kernels, streamed(): pl.pallas_call(functools.partial(stream_kernel, n, dps, capacity, block,...  133 us
    unnamed x6, local copies, waits for them, and re-layouts  3.75 us

profile of v1, /device:TPU:0, one launch (start us, length us, event | category | flops | bytes accessed | tf_op | source)
XLA Modules:
  0.0 139.3 jit_solution(14349881038118620291)
XLA Ops:
  0.6 0.0 copy-start.1
  0.6 0.0 copy-start.3
  0.6 133.1 %shard_map.70 = (bf16[512,2048]{1,0:T(8,128)(2,1)}, s32[1,512]{1,0:T(1,128)S(1)}, s32[8,128]{1,0:T(8,128)}) custom-call(s32[1,512]{1,0:T(1,128)} %bitcast.47, bf16[512,2048]{1,0:T(8,128)(2,1)} %tok_hbm.1, bf16[1,2048,768]{2,1,0:T(8,128)(2,1)} %gate_hbm.1, bf16[1,2048,768]{2,1,0:T(8,128)(2,1)} %up_hbm.1, bf16[1,768,2048]{2,1,0:T(8,128)(2,1)} %down_hbm.1), custom_call_target="tpu_custom_call" | custom-call | tf_op jit(solution)/shard_map/pallas_call | solution.py:930
  133.7 1.2 slice.9
  135.6 0.0 copy-done.1
  135.6 0.0 copy-done.3
  135.6 3.2 %copy.33 = bf16[512,2048]{1,0:T(8,128)(2,1)} copy(bf16[512,2048]{1,0:T(8,128)(2,1)} %get-tuple-element.200) | data formatting | bytes 4194304
  138.8 0.6 copy.34
  (1 shorter events, 0.0 us)
Async XLA Ops:
  0.6 134.9 %copy-start.1 = (bf16[1,2048,768]{2,1,0:T(8,128)(2,1)S(1)}, bf16[1,2048,768]{2,1,0:T(8,128)(2,1)}, u32[]{:S(2)}) copy-start(bf16[1,2048,768]{2,1,0:T(8,128)(2,1)} %gate_hbm.1) | copy-start | bytes 9437188
  0.6 134.9 %copy-start.3 = (s32[512,1]{0,1:T(1,128)S(1)}, s32[512,1]{0,1:T(1,128)}, u32[]{:S(2)}) copy-start(s32[512,1]{0,1:T(1,128)} %param.12) | copy-start | bytes 6148

commit v2 on v1

--- a/solution.py
+++ b/solution.py
@@ -11,7 +11,7 @@
 F32 = jnp.float32
 BF16 = jnp.bfloat16
 LANES = 128
-NEAR_BLOCKS, FAR_BLOCKS, GO_BLOCKS, DELAY = 18, 19, 13, 3
+LAG, HOLD = 3, 9
 
 
 def spread(step, n):
@@ -350,22 +350,24 @@
     return (mixed.astype(jnp.bfloat16), global_slot)
 
 
-NEAR_ORDER = {
-    "A": (("go", "o", "p"), ("go", "o", "q"), ("go", "o", "i"),
-          ("ret", "o", "i"), ("ret", "o", "p"), ("ret", "o", "q")),
-    "M": (("go", "i", "p"), ("go", "i", "q"), ("go", "o", "p"), ("go", "o", "q"),
-          ("ret", "i", "p"), ("ret", "i", "q"), ("ret", "o", "p"), ("ret", "o", "q")),
-    "B": (("go", "i", "o"), ("go", "p", "o"), ("go", "q", "o"),
-          ("ret", "i", "o"), ("ret", "p", "o"), ("ret", "q", "o")),
+RUN_ORDER = {
+    "A": ("go op", "go oq", "go oi", "ret op", "ret oq", "ret oi"),
+    "M": (
+        "go ip", "go iq", "go oq", "go op", "ret ip", "ret op", "ret iq", "ret oq",
+    ),
+    "B": ("go io", "go po", "go qo", "ret io", "ret po", "ret qo"),
 }
 FLIP = {"o": "q", "i": "p", "p": "i", "q": "o"}
 FAR_KEY = 4096
 LOCAL_KEY = 8192
 
 
-def lay_streams(rows_of, block, delay):
+def lay_streams(rows_of, block):
     place, end = {}, {}
-    queue = {(s, h): list(NEAR_ORDER[s]) for s in "AMB" for h in (0, 1)}
+    queue = {
+        (s, h): [(run[:-3], run[-2], run[-1]) for run in RUN_ORDER[s]]
+        for s in "AMB" for h in (0, 1)
+    }
     zero = jnp.zeros((1, LANES), jnp.int32)
     for name in queue:
         end[name] = zero
@@ -374,23 +376,29 @@
             while runs:
                 kind, a, b = runs[0]
                 fa, fb = FLIP[a], FLIP[b]
-                need = None
+                need, result = None, kind == "ret"
                 if s == "A" and kind == "ret":
-                    need = (("B", h, "go", b, a), 3 + delay)
+                    need = ("B", h, "go", b, a)
                 elif s == "M" and a == "o":
-                    need = (("A", h, kind, a, b), 2)
+                    need, result = ("A", h, kind, a, b), False
                 elif s == "M" and kind == "ret":
-                    need = (("M", 1 - h, "go", fb, fa), 3)
+                    need = ("M", 1 - h, "go", fb, fa)
                 elif s == "B" and a != "i":
-                    need = (("M", 1 - h, kind, fa, fb), 2 - delay)
+                    need, result = ("M", 1 - h, kind, fa, fb), False
                 elif s == "B" and kind == "ret":
-                    need = (("A", h, "go", b, a), 3 - delay)
-                if need is not None and need[0] not in place:
+                    need = ("A", h, "go", b, a)
+                if need is not None and need not in place:
                     break
                 size = rows_of(h, a, b) if kind == "go" else rows_of(h, b, a)
                 first = end[(s, h)]
                 if need is not None:
-                    ready = place[need[0]][0] + block * need[1]
+                    there = place[need][0]
+                    ready = there + block * LAG
+                    if result:
+                        ready = jnp.maximum(
+                            ready + block * 2,
+                            lax.shift_right_logical(there, 1) + block * (HOLD + 1),
+                        )
                     first = jnp.where(size > 0, jnp.maximum(first, ready), first)
                 place[(s, h, kind, a, b)] = (first, size)
                 end[(s, h)] = first + size
@@ -399,7 +407,7 @@
 
 
 def stream_kernel(
-    n, dps, capacity, block, near_blocks, far_blocks, go_blocks, delay,
+    n, dps, capacity, block, near_blocks, far_blocks, go_blocks, back_blocks,
     row_ids, tok_hbm, gate_hbm, up_hbm, down_hbm,
     out_ref, slot_ref, flag_ref,
     gate_ref, up_ref, down_ref, pool, inbox, outbox,
@@ -418,14 +426,16 @@
     roles = {"o": 3 * half, "i": 1 + half, "p": 2 - half, "q": 3 - 3 * half}
     inner = chip == roles["i"]
     is_inner = inner.astype(jnp.int32)
-    is_outer = 1 - is_inner
+    near_limit = near_blocks - LAG * (1 - is_inner)
     near_dev = me + 2 - 4 * lax.rem(chip, 2)
     far_dev = 2 * (3 - chip) + core
     pair_dev = me + 1 - 2 * core
     two = 2 * block
     blocks = inbox.shape[0] // two
-    steps = max(far_blocks, near_blocks + delay)
-    local_at = tok + blocks * two
+    pair = 2 * two
+    steps = near_blocks
+    tok_at = 2 * pair
+    base = tok_at + tok
     piece = min(width, 512)
     ring = outbox.shape[0]
 
@@ -438,7 +448,7 @@
     def dot(a, b):
         return jnp.dot(a, b, preferred_element_type=F32)
 
-    load_tok = pltpu.make_async_copy(tok_hbm, pool.at[pl.ds(0, tok)], tok_sem.at[0])
+    load_tok = pltpu.make_async_copy(tok_hbm, pool.at[pl.ds(tok_at, tok)], tok_sem.at[0])
     load_tok.start()
     mine_down = pl.ds(pl.multiple_of(core * hidden, hidden), hidden)
     pairs = (
@@ -489,9 +499,15 @@
 
     ids_row = row_ids[...]
     hot_row = (ids_row == iota((n, tok), 0)).astype(F32)
-    before_row = dot(hot_row.astype(BF16), ones(iota((tok, tok), 0) < iota((tok, tok), 1)))
+    earlier = ones(iota((LANES, LANES), 0) < iota((LANES, LANES), 1))
+    ahead, mine = [], jnp.zeros((n, 1), F32)
+    for lo in range(0, tok, LANES):
+        hot = hot_row[:, lo : lo + LANES]
+        ahead.append(dot(hot.astype(BF16), earlier) + mine)
+        mine = mine + jnp.sum(hot, axis=1, keepdims=True)
+    before_row = jnp.concatenate(ahead, axis=1)
     rank_row = jnp.sum(before_row * hot_row, axis=0, keepdims=True).astype(jnp.int32)
-    mine = jnp.broadcast_to(jnp.sum(hot_row, axis=1, keepdims=True), (n, LANES))
+    mine = jnp.broadcast_to(mine, (n, LANES))
     counts[...] = mine.astype(jnp.int32)
     row8 = iota((n, n), 0)
     shift = ones((iota((n, n), 1) + 1 == row8) & (lax.rem(row8, 2) == 1))
@@ -509,10 +525,10 @@
     to_o = jnp.where(inner, zero1, LOCAL_KEY)
     to_i = jnp.where(inner, LOCAL_KEY, own_rows("p") + own_rows("q"))
     to_p = jnp.where(inner, zero1 + FAR_KEY, 0)
-    to_q = own_rows("p") + jnp.where(inner, FAR_KEY, 0)
+    to_q = own_rows("p") + to_p
     key = jnp.zeros((1, tok), jnp.int32)
-    for role, base in (("o", to_o), ("i", to_i), ("p", to_p), ("q", to_q)):
-        key = jnp.where(pair_row == roles[role], base + pair_rank, key)
+    for role, to in (("o", to_o), ("i", to_i), ("p", to_p), ("q", to_q)):
+        key = jnp.where(pair_row == roles[role], to + pair_rank, key)
     tok_key[...] = key
 
     def near_copy(j, slot):
@@ -545,67 +561,59 @@
             device_id={"dp": dest}, device_id_type=MESH,
         )
 
+    def far_on(k):
+        return inner & (k < far_blocks)
+
     def sent(k):
         slot = lax.rem(k, ring)
-        near_at = k - delay * is_inner
-
-        @pl.when((near_at >= 0) & (near_at < near_blocks))
+
+        @pl.when(k < near_limit)
         def _():
-            near_copy(near_at, slot).wait_send()
-
-        @pl.when(inner & (k < far_blocks))
+            near_copy(k, slot).wait_send()
+
+        @pl.when(far_on(k))
         def _():
             far_copy(k, slot).wait_send()
 
-    def send(k, low, high):
+    def pack(k, low, high):
         slot = lax.rem(k, ring)
-        near_at = k - delay * is_inner
-
-        @pl.when(k >= ring)
+        row = iota((two, 1), 0)
+        want = jnp.where(row < block, k * block + row, FAR_KEY + k * block + row - block)
+        picks = []
+        if low < base:
+            picks.append(ones(want == tok_key[...]))
+        if high > base:
+            picks.append(ones(want == in_key[:, max(low, base) - base : high - base]))
+        pick = picks[0] if len(picks) == 1 else jnp.concatenate(picks, axis=1)
+        for at in range(0, width, piece):
+            outbox[slot, :, at : at + piece] = dot(
+                pick, pool[low:high, at : at + piece]
+            ).astype(BF16)
+
+    def launch(k):
+        slot = lax.rem(k, ring)
+
+        @pl.when(k < near_limit)
         def _():
-            sent(k - ring)
-
-        @pl.when(inner | (k < near_blocks))
-        def _():
-            row = iota((two, 1), 0)
-            want = jnp.where(
-                row < block, near_at * block + row, FAR_KEY + k * block + row - block
-            )
-            picks = []
-            if low < tok:
-                picks.append(ones(want == tok_key[...]))
-            if high > tok:
-                picks.append(ones(want == in_key[:, max(low, tok) - tok : high - tok]))
-            pick = picks[0] if len(picks) == 1 else jnp.concatenate(picks, axis=1)
-            for at in range(0, width, piece):
-                outbox[slot, :, at : at + piece] = dot(
-                    pick, pool[low:high, at : at + piece]
-                ).astype(BF16)
-
-        @pl.when((near_at >= 0) & (near_at < near_blocks))
-        def _():
-            near_copy(near_at, slot).start()
-
-        @pl.when(inner & (k < far_blocks))
+            near_copy(k, slot).start()
+
+        @pl.when(far_on(k))
         def _():
             far_copy(k, slot).start()
 
     def arrive(b):
         at = pl.multiple_of(b * two, two)
-
-        @pl.when((b >= 0) & (b < near_blocks))
-        def _():
-            near_copy(b, 0).wait_recv()
-            pool[pl.ds(tok + at, block), :] = inbox[pl.ds(at, block), :]
-
-        @pl.when(inner & (b >= 0) & (b < far_blocks))
+        near_copy(b, 0).wait_recv()
+        pool[pl.ds(base + at, block), :] = inbox[pl.ds(at, block), :]
+
+        @pl.when(far_on(b))
         def _():
             far_copy(b, 0).wait_recv()
-            pool[pl.ds(tok + at + block, block), :] = inbox[pl.ds(at + block, block), :]
+            pool[pl.ds(base + at + block, block), :] = inbox[pl.ds(at + block, block), :]
 
     def ffn(rows, code):
         parts = []
-        wide = jnp.broadcast_to(code, (two, hidden))
+        wide = jnp.broadcast_to(code, (pair, hidden))
         for parity in (0, 1):
             gate = dot(rows, gate_ref[parity])
             up = dot(rows, up_ref[parity])
@@ -616,30 +624,30 @@
             dot(act, down_ref[:, at : at + piece]) for at in range(0, width, piece)
         ]
 
-    spare = pool.at[pl.ds(tok, blocks * two)]
+    load_tok.wait()
+    pack(0, tok_at, base)
+    pl.semaphore_wait(barrier, n + dps - 2)
+    launch(0)
+
+    def tell(i, c):
+        count(lax.rem(me + i, n), me).start()
+        return c
+
+    lax.fori_loop(1, n, tell, 0)
+    for copy in share:
+        copy.start()
+    for k in range(1, LAG):
+        pack(k, tok_at, base)
+        launch(k)
+    count_all[me] = counts[...]
+
+    spare = pool.at[pl.ds(base, blocks * two)]
 
     def clear(i, c):
         spare[pl.ds(pl.multiple_of(i * two, two), two), :] = jnp.zeros((two, width), BF16)
         return c
 
     lax.fori_loop(0, blocks, clear, 0)
-    load_tok.wait()
-    pl.semaphore_wait(barrier, n + dps - 2)
-
-    def tell(i, c):
-        count(lax.rem(me + i, n), me).start()
-        return c
-
-    lax.fori_loop(1, n, tell, 0)
-    count_all[me] = counts[...]
-
-    def first_steps(k, c):
-        send(k, 0, tok)
-        return c
-
-    lax.fori_loop(0, 2, first_steps, 0)
-    for copy in share:
-        copy.start()
 
     def heard(i, c):
         count(me, lax.rem(me + i, n)).wait_recv()
@@ -658,18 +666,20 @@
     def even(a):
         return count_all[2 * roles[a] + core, pl.ds(2 * chip, 1), :][:, 0:1]
 
-    place, ends = lay_streams(rows_of(core), block, delay)
+    place, ends = lay_streams(rows_of(core), block)
     over = jnp.zeros((1, LANES), jnp.int32)
     for lane_place, lane_ends in (
-        (place, ends), lay_streams(rows_of(1 - core), block, delay)
+        (place, ends), lay_streams(rows_of(1 - core), block)
     ):
         for (s, _), end in lane_ends.items():
-            limit = (far_blocks if s == "M" else near_blocks) * block
+            limit = {"A": near_blocks - LAG, "M": far_blocks, "B": near_blocks}[s] * block
             over = jnp.maximum(over, (end > limit).astype(jnp.int32))
         for name, (first, size) in lane_place.items():
             if name[2] == "go":
-                late = (first + size > go_blocks * block) & (size > 0)
-                over = jnp.maximum(over, late.astype(jnp.int32))
+                bad = (first + size > go_blocks * block) & (size > 0)
+            else:
+                bad = (first < back_blocks * block) & (size > 0)
+            over = jnp.maximum(over, bad.astype(jnp.int32))
 
     def at(name):
         first, size = place[name]
@@ -728,23 +738,29 @@
         split = jnp.where(inner, even(a_in), even(a_out))
         mine_runs.append((first, size, split, far_side * is_inner))
 
-    def mark(b):
-        row = iota((two, 1), 0)
-        side = lax.div(row, block)
-        spot = b * block + lax.rem(row, block)
-        code = jnp.zeros((two, 1), jnp.int32)
+    mine_pairs = go_blocks // 2
+
+    def mark(m):
+        row = iota((pair, 1), 0)
+        side = lax.div(lax.rem(row, two), block)
+        spot = (2 * m + lax.div(row, two)) * block + lax.rem(row, block)
+        code = jnp.zeros((pair, 1), jnp.int32)
         for first, size, split, which in mine_runs:
             hit = (spot >= first) & (spot < first + size) & (side == which)
             code = jnp.where(hit, jnp.where(spot - first >= split, 2, 1), code)
-        return code
-
-    home = zero1 + local_at
+        rank = (m - mine_pairs) * pair + row
+        first = counts[pl.ds(2 * chip, 1), :][:, 0:1]
+        both = first + counts[pl.ds(2 * chip + 1, 1), :][:, 0:1]
+        local = jnp.where(rank < both, jnp.where(rank >= first, 2, 1), 0)
+        return jnp.where(m < mine_pairs, code, local)
+
+    home = zero1
 
     def pool_at(run, side):
         def get(rank):
             spot = start(run) + rank
             return (
-                tok + lax.div(spot, block) * two + lax.rem(spot, block) + side * block
+                base + lax.div(spot, block) * two + lax.rem(spot, block) + side * block
             )
 
         return get
@@ -785,58 +801,75 @@
 
     lax.fori_loop(1, dps, tell_dp, 0)
 
-    def work(b):
-        at = pl.multiple_of(tok + b * two, two)
-        code = mark(b)
-        done = ffn(pool[pl.ds(at, two), :], code)
-        wide = jnp.broadcast_to(code, (two, piece))
+    def work(m):
+        at = jnp.where(m < mine_pairs, base + m * pair, (m - mine_pairs) * pair)
+        at = pl.multiple_of(at, pair)
+        code = mark(m)
+        done = ffn(pool[pl.ds(at, pair), :], code)
+        wide = jnp.broadcast_to(code, (pair, piece))
         for i, part in enumerate(done):
             cols = slice(i * piece, (i + 1) * piece)
-            raw = pool[pl.ds(at, two), cols].astype(F32)
-            pool[pl.ds(at, two), cols] = jnp.where(wide > 0, part, raw).astype(BF16)
-
-    def step(low, high, busy):
+            raw = pool[pl.ds(at, pair), cols].astype(F32)
+            pool[pl.ds(at, pair), cols] = jnp.where(wide > 0, part, raw).astype(BF16)
+
+    own_end = tok // block
+    cuts = [LAG, LAG + 4, LAG + 8, own_end]
+    while cuts[-1] < steps:
+        ahead = (cuts[-1] - LAG) // 4 * 4 + 4 + LAG
+        cuts.append(min(steps, ahead))
+
+    def step(busy, first, last):
         def run(k, c):
-            b = k - 2 - delay * is_outer
-            arrive(b)
-            send(k, low, high)
+            arrive(k - LAG)
+
+            @pl.when(k >= ring)
+            def _():
+                sent(k - ring)
+
+            for lo, hi in zip(cuts[:-1], cuts[1:]):
+                if hi <= first or lo >= last:
+                    continue
+
+                @pl.when((k >= lo) & (k < hi) & (k < near_limit))
+                def _():
+                    pack(
+                        k, tok_at if lo < own_end else base, base + (hi - LAG) * two
+                    )
+
+            launch(k)
             if busy:
-                @pl.when((b >= 0) & (b < go_blocks))
+                m = jnp.where(k < switch, k - HOLD, lax.div(k - LAG - 1, 2))
+
+                @pl.when(
+                    ((k < switch) | (lax.rem(k - LAG, 2) == 1)) & (m < mine_pairs + 2)
+                )
                 def _():
-                    work(b)
+                    work(m)
 
             return c
 
-        return run
-
-    def local(i, c):
-        rank = i * two + iota((two, 1), 0)
-        rows = dot(ones(rank + LOCAL_KEY == tok_key[...]), pool[0:tok, :]).astype(BF16)
-        e = 2 * chip
-        first = counts[pl.ds(e, 1), :][:, 0:1]
-        both = first + counts[pl.ds(e + 1, 1), :][:, 0:1]
-        code = jnp.where(rank < both, jnp.where(rank >= first, 2, 1), 0)
-        at = pl.multiple_of(local_at + i * two, two)
-        for j, part in enumerate(ffn(rows, code)):
-            pool[pl.ds(at, two), j * piece : (j + 1) * piece] = part.astype(BF16)
-        return c
-
-    cut = tok // block
-    last = go_blocks + 2 + delay
-    lax.fori_loop(2, 3, step(0, tok + two, False), 0)
+        lax.fori_loop(first, last, run, 0)
+
+    switch = 2 * HOLD - LAG
+    step(False, LAG, HOLD)
+
+    def gather_local(i, c):
+        rank = i * pair + iota((pair, 1), 0)
+        at = pl.multiple_of(i * pair, pair)
+        pick = ones(rank + LOCAL_KEY == tok_key[...])
+        for col in range(0, width, piece):
+            pool[pl.ds(at, pair), col : col + piece] = dot(
+                pick, pool[tok_at:base, col : col + piece]
+            ).astype(BF16)
+        return c
+
+    lax.fori_loop(0, 2, gather_local, 0)
+
     for copy in own:
         copy.wait()
     for copy in arriving:
         copy.wait_recv()
-
-    @pl.when(inner)
-    def _():
-        work(0)
-
-    lax.fori_loop(3, cut, step(0, tok + (cut - 2) * two, True), 0)
-    lax.fori_loop(cut, last, step(tok, tok + (last - 2) * two, True), 0)
-    lax.fori_loop(last, steps, step(tok, local_at, False), 0)
-    lax.fori_loop(0, 2, local, 0)
+    step(True, HOLD, steps)
 
     def heard_dp(i, c):
         total(group, lax.rem(group + i, dps)).wait_recv()
@@ -853,17 +886,17 @@
 
     outer, most = lax.fori_loop(0, dps, add_dp, (zero, over))
     offset = before + outer
-    flag_ref[...] = most
+    flag_ref[...] = most[0:1, 0:1]
     slot = jnp.sum(
         hot_row * offset[:, 0:1].astype(F32), axis=0, keepdims=True
     ).astype(jnp.int32) + rank_row
     slot_ref[...] = slot
-    from_row = jnp.where(slot < capacity, from_row, 0)
+    from_row = jnp.where(slot < capacity, from_row, -1)
     position[...] = jnp.transpose(
         jnp.broadcast_to(from_row, (8, tok)).astype(F32)
     )[:, 0:1].astype(jnp.int32)
 
-    span = 4 * two
+    span = 8 * two
 
     def combine(at, size, first):
         pick = ones(position[...] == iota((1, size), 1) + at)
@@ -875,22 +908,25 @@
             else:
                 out_ref[:, col : col + piece] += part
 
-    seen = (steps - 2 - delay) * two // span
-    combine(tok, span, True)
+    combine(0, tok_at, True)
+    seen = base + (steps - LAG) * two
+    whole_at = base + back_blocks * two
+    spans = (seen - whole_at) // span
 
     def combine_step(c, carry):
-        combine(tok + c * span, span, False)
+        combine(whole_at + c * span, span, False)
         return carry
 
-    lax.fori_loop(1, seen, combine_step, 0)
+    lax.fori_loop(0, spans, combine_step, 0)
+    if whole_at + spans * span < seen:
+        combine(whole_at + spans * span, seen - whole_at - spans * span, False)
 
     def late(b, c):
         arrive(b)
         return c
 
-    lax.fori_loop(steps - 2 - delay * is_outer, near_blocks, late, 0)
-    rest = tok + seen * span
-    combine(rest, pool.shape[0] - rest, False)
+    lax.fori_loop(steps - LAG, near_blocks - LAG * is_inner, late, 0)
+    combine(seen, pool.shape[0] - seen, False)
 
     def flush(k, c):
         sent(k)
@@ -919,9 +955,12 @@
     n = lax.axis_size("expert")
     dps = lax.axis_size("dp")
     capacity = tok * dps
-    block = tok // n
-    near_blocks, far_blocks, go_blocks, delay = NEAR_BLOCKS, FAR_BLOCKS, GO_BLOCKS, DELAY
-    blocks = max(near_blocks, far_blocks)
+    block = tok // (2 * n)
+    far_blocks = 9 * n // 2
+    near_blocks = far_blocks + LAG
+    go_blocks = 13 * n // 4
+    back_blocks = n
+    blocks = near_blocks
     ring = 4
     vmem = pl.BlockSpec(memory_space=pltpu.VMEM)
     anywhere = pl.BlockSpec(memory_space=pltpu.MemorySpace.HBM)
@@ -929,12 +968,13 @@
     table = pltpu.VMEM((n, LANES), jnp.int32)
     mixed, slot, flag = pl.pallas_call(
         functools.partial(
-            stream_kernel, n, dps, capacity, block, near_blocks, far_blocks, go_blocks, delay
+            stream_kernel, n, dps, capacity, block, near_blocks, far_blocks, go_blocks,
+            back_blocks,
         ),
         out_shape=(
             jax.ShapeDtypeStruct((tok, width), BF16),
             jax.ShapeDtypeStruct((1, tok), jnp.int32),
-            jax.ShapeDtypeStruct((n, LANES), jnp.int32),
+            jax.ShapeDtypeStruct((1, 1), jnp.int32),
         ),
         in_specs=[vmem, anywhere, anywhere, anywhere, anywhere],
         out_specs=(vmem, vmem, vmem),
@@ -942,7 +982,7 @@
             pltpu.VMEM((2, width, hidden), BF16),
             pltpu.VMEM((2, width, hidden), BF16),
             pltpu.VMEM((2 * hidden, width), BF16),
-            pltpu.VMEM((tok + 2 * block * blocks + 4 * block, width), BF16),
+            pltpu.VMEM((8 * block + tok + 2 * block * blocks, width), BF16),
             pltpu.VMEM((2 * block * blocks, width), BF16),
             pltpu.VMEM((ring, 2 * block, width), BF16),
             pltpu.VMEM((1, tok), jnp.int32),

time: 140 us -> 129 us (0.921)
  Pallas kernels: 133 us -> 124 us
    pallas_call x1, Pallas kernels: 133 us -> 124 us  [streamed(): pl.pallas_call(functools.partial(stream_kernel, n, dps, capacity, block,...]
where the time goes in v2:
time: 129 us
  Pallas kernels  124 us (96%)
  local copies, waits for them, and re-layouts  3.75 us (3%)
  between operations  1.37 us (1%)
    pallas_call x1, Pallas kernels, streamed(): pl.pallas_call(functools.partial(stream_kernel, n, dps, capacity, block,...  124 us
    unnamed x6, local copies, waits for them, and re-layouts  3.75 us

profile of v2, /device:TPU:0, one launch (start us, length us, event | category | flops | bytes accessed | tf_op | source)
XLA Modules:
  0.0 129.2 jit_solution(13157448727856618171)
XLA Ops:
  0.6 0.0 copy-start.1
  0.6 0.0 copy-start.3
  0.6 124.0 %shard_map.70 = (bf16[512,2048]{1,0:T(8,128)(2,1)}, s32[1,512]{1,0:T(1,128)S(1)}, s32[1,1]{1,0:T(1,128)}) custom-call(s32[1,512]{1,0:T(1,128)} %bitcast.47, bf16[512,2048]{1,0:T(8,128)(2,1)} %tok_hbm.1, bf16[1,2048,768]{2,1,0:T(8,128)(2,1)} %gate_hbm.1, bf16[1,2048,768]{2,1,0:T(8,128)(2,1)} %up_hbm.1, bf16[1,768,2048]{2,1,0:T(8,128)(2,1)} %down_hbm.1), custom_call_target="tpu_custom_call" | custom-call | tf_op jit(solution)/shard_map/pallas_call | solution.py:969
  125.4 0.0 copy-done.1
  125.4 0.0 copy-done.3
  125.4 3.2 %copy.33 = bf16[512,2048]{1,0:T(8,128)(2,1)} copy(bf16[512,2048]{1,0:T(8,128)(2,1)} %get-tuple-element.200) | data formatting | bytes 4194304
  128.6 0.6 copy.34
  (1 shorter events, 0.0 us)
Async XLA Ops:
  0.6 124.8 %copy-start.1 = (bf16[1,2048,768]{2,1,0:T(8,128)(2,1)S(1)}, bf16[1,2048,768]{2,1,0:T(8,128)(2,1)}, u32[]{:S(2)}) copy-start(bf16[1,2048,768]{2,1,0:T(8,128)(2,1)} %gate_hbm.1) | copy-start | bytes 9437188
  0.6 124.8 %copy-start.3 = (s32[512,1]{0,1:T(1,128)S(1)}, s32[512,1]{0,1:T(1,128)}, u32[]{:S(2)}) copy-start(s32[512,1]{0,1:T(1,128)} %param.12) | copy-start | bytes 6148

commit v3 on v2

--- a/solution.py
+++ b/solution.py
@@ -11,7 +11,7 @@
 F32 = jnp.float32
 BF16 = jnp.bfloat16
 LANES = 128
-LAG, HOLD = 3, 9
+LAG, HOLD, REST = 3, 7, 23
 
 
 def spread(step, n):
@@ -399,6 +399,8 @@
                             ready + block * 2,
                             lax.shift_right_logical(there, 1) + block * (HOLD + 1),
                         )
+                    if s == "B":
+                        ready -= block * jnp.clip(ready // block - REST, 0, LAG)
                     first = jnp.where(size > 0, jnp.maximum(first, ready), first)
                 place[(s, h, kind, a, b)] = (first, size)
                 end[(s, h)] = first + size
@@ -426,17 +428,17 @@
     roles = {"o": 3 * half, "i": 1 + half, "p": 2 - half, "q": 3 - 3 * half}
     inner = chip == roles["i"]
     is_inner = inner.astype(jnp.int32)
-    near_limit = near_blocks - LAG * (1 - is_inner)
     near_dev = me + 2 - 4 * lax.rem(chip, 2)
     far_dev = 2 * (3 - chip) + core
     pair_dev = me + 1 - 2 * core
     two = 2 * block
     blocks = inbox.shape[0] // two
     pair = 2 * two
-    steps = near_blocks
+    steps = far_blocks + LAG
+    b_blocks = far_blocks
     tok_at = 2 * pair
     base = tok_at + tok
-    piece = min(width, 512)
+    piece = min(width, 1024)
     ring = outbox.shape[0]
 
     def iota(shape, axis):
@@ -561,15 +563,22 @@
             device_id={"dp": dest}, device_id_type=MESH,
         )
 
+    def near_at(k, rests):
+        return k - rests * jnp.where(k < REST + LAG, 0, LAG)
+
+    def near_on(k, rests):
+        idle = rests * jnp.where((k >= REST) & (k < REST + LAG), 1, 0)
+        return (idle == 0) & (k < near_blocks + rests * (steps - near_blocks))
+
     def far_on(k):
         return inner & (k < far_blocks)
 
     def sent(k):
         slot = lax.rem(k, ring)
 
-        @pl.when(k < near_limit)
+        @pl.when(near_on(k, is_inner))
         def _():
-            near_copy(k, slot).wait_send()
+            near_copy(near_at(k, is_inner), slot).wait_send()
 
         @pl.when(far_on(k))
         def _():
@@ -578,7 +587,9 @@
     def pack(k, low, high):
         slot = lax.rem(k, ring)
         row = iota((two, 1), 0)
-        want = jnp.where(row < block, k * block + row, FAR_KEY + k * block + row - block)
+        want = jnp.where(
+            row < block, near_at(k, is_inner) * block + row, FAR_KEY + k * block + row - block
+        )
         picks = []
         if low < base:
             picks.append(ones(want == tok_key[...]))
@@ -593,22 +604,28 @@
     def launch(k):
         slot = lax.rem(k, ring)
 
-        @pl.when(k < near_limit)
+        @pl.when(near_on(k, is_inner))
         def _():
-            near_copy(k, slot).start()
+            near_copy(near_at(k, is_inner), slot).start()
 
         @pl.when(far_on(k))
         def _():
             far_copy(k, slot).start()
 
-    def arrive(b):
+    def take(b):
         at = pl.multiple_of(b * two, two)
         near_copy(b, 0).wait_recv()
         pool[pl.ds(base + at, block), :] = inbox[pl.ds(at, block), :]
 
-        @pl.when(far_on(b))
+    def arrive(k):
+        @pl.when(near_on(k, 1 - is_inner))
         def _():
-            far_copy(b, 0).wait_recv()
+            take(near_at(k, 1 - is_inner))
+
+        @pl.when(far_on(k))
+        def _():
+            far_copy(k, 0).wait_recv()
+            at = pl.multiple_of(k * two, two)
             pool[pl.ds(base + at + block, block), :] = inbox[pl.ds(at + block, block), :]
 
     def ffn(rows, code):
@@ -672,11 +689,12 @@
         (place, ends), lay_streams(rows_of(1 - core), block)
     ):
         for (s, _), end in lane_ends.items():
-            limit = {"A": near_blocks - LAG, "M": far_blocks, "B": near_blocks}[s] * block
+            limit = {"A": near_blocks, "M": far_blocks, "B": b_blocks}[s] * block
             over = jnp.maximum(over, (end > limit).astype(jnp.int32))
         for name, (first, size) in lane_place.items():
             if name[2] == "go":
-                bad = (first + size > go_blocks * block) & (size > 0)
+                limit = (REST if name[0] == "B" else go_blocks) * block
+                bad = (first + size > limit) & (size > 0)
             else:
                 bad = (first < back_blocks * block) & (size > 0)
             over = jnp.maximum(over, bad.astype(jnp.int32))
@@ -818,6 +836,21 @@
         ahead = (cuts[-1] - LAG) // 4 * 4 + 4 + LAG
         cuts.append(min(steps, ahead))
 
+    span = 8 * two
+
+    def combine(at, size, first):
+        pick = ones(position[...] == iota((1, size), 1) + at)
+        rows = pl.ds(at if isinstance(at, int) else pl.multiple_of(at, two), size)
+        for col in range(0, width, piece):
+            part = dot(pick, pool[rows, col : col + piece]).astype(BF16)
+            if first:
+                out_ref[:, col : col + piece] = part
+            else:
+                out_ref[:, col : col + piece] += part
+
+    whole_at = base + back_blocks * two
+    early = REST // 8 - 1
+
     def step(busy, first, last):
         def run(k, c):
             arrive(k - LAG)
@@ -830,7 +863,7 @@
                 if hi <= first or lo >= last:
                     continue
 
-                @pl.when((k >= lo) & (k < hi) & (k < near_limit))
+                @pl.when((k >= lo) & (k < hi) & (inner | (k < near_blocks)))
                 def _():
                     pack(
                         k, tok_at if lo < own_end else base, base + (hi - LAG) * two
@@ -869,8 +902,6 @@
         copy.wait()
     for copy in arriving:
         copy.wait_recv()
-    step(True, HOLD, steps)
-
     def heard_dp(i, c):
         total(group, lax.rem(group + i, dps)).wait_recv()
         return c
@@ -896,37 +927,25 @@
         jnp.broadcast_to(from_row, (8, tok)).astype(F32)
     )[:, 0:1].astype(jnp.int32)
 
-    span = 8 * two
-
-    def combine(at, size, first):
-        pick = ones(position[...] == iota((1, size), 1) + at)
-        rows = pl.ds(at if isinstance(at, int) else pl.multiple_of(at, two), size)
-        for col in range(0, width, piece):
-            part = dot(pick, pool[rows, col : col + piece]).astype(BF16)
-            if first:
-                out_ref[:, col : col + piece] = part
-            else:
-                out_ref[:, col : col + piece] += part
-
+    step(True, HOLD, steps)
     combine(0, tok_at, True)
-    seen = base + (steps - LAG) * two
-    whole_at = base + back_blocks * two
-    spans = (seen - whole_at) // span
 
     def combine_step(c, carry):
         combine(whole_at + c * span, span, False)
         return carry
 
-    lax.fori_loop(0, spans, combine_step, 0)
-    if whole_at + spans * span < seen:
-        combine(whole_at + spans * span, seen - whole_at - spans * span, False)
+    lax.fori_loop(0, early + 2, combine_step, 0)
+    rest = whole_at + (early + 2) * span
 
     def late(b, c):
-        arrive(b)
-        return c
-
-    lax.fori_loop(steps - LAG, near_blocks - LAG * is_inner, late, 0)
-    combine(seen, pool.shape[0] - seen, False)
+        take(b)
+        return c
+
+    lax.fori_loop(
+        jnp.where(inner, steps - LAG, steps - 2 * LAG),
+        jnp.where(inner, near_blocks, b_blocks), late, 0,
+    )
+    combine(rest, pool.shape[0] - rest, False)
 
     def flush(k, c):
         sent(k)
@@ -947,6 +966,29 @@
         return c
 
     lax.fori_loop(1, dps, drain_dp, 0)
+
+
+def settle_kernel(rows_in, slot_in, rows_out, slot_out):
+    rows_out[...] = rows_in[...]
+    slot_out[...] = slot_in[...]
+
+
+def settle_outputs(mixed, slot):
+    tok, width = mixed.shape
+    parts = 2
+    rows = pl.BlockSpec((tok // parts, width), lambda i: (i, 0))
+    whole = pl.BlockSpec((1, tok), lambda i: (0, 0))
+    mixed, slot = pl.pallas_call(
+        settle_kernel,
+        grid=(parts,),
+        out_shape=(
+            jax.ShapeDtypeStruct(mixed.shape, mixed.dtype),
+            jax.ShapeDtypeStruct(slot.shape, slot.dtype),
+        ),
+        in_specs=[rows, whole],
+        out_specs=(rows, whole),
+    )(mixed, slot)
+    return mixed, slot.reshape(tok)
 
 
 def streamed(tokens, expert_ids, gate_proj, up_proj, down_proj):
@@ -957,7 +999,7 @@
     capacity = tok * dps
     block = tok // (2 * n)
     far_blocks = 9 * n // 2
-    near_blocks = far_blocks + LAG
+    near_blocks = far_blocks + 1
     go_blocks = 13 * n // 4
     back_blocks = n
     blocks = near_blocks
@@ -1003,7 +1045,7 @@
     return lax.cond(
         flag[0, 0] > 0,
         lambda: padded(tokens, expert_ids, gate_proj, up_proj, down_proj),
-        lambda: (mixed, slot.reshape(tok)),
+        lambda: tuple(settle_outputs(mixed, slot)),
     )
 
 

time: 129 us -> 125 us (0.969)
  local copies, waits for them, and re-layouts: 3.75 us -> 0.01 us
    unnamed x6 -> x4, local copies, waits for them, and re-layouts: 3.75 us -> 0.01 us
    pallas_call x1, Pallas kernels: 124 us -> 121 us  [streamed(): pl.pallas_call(functools.partial(stream_kernel, n, dps, capacity, block,...]
    pallas_call x0 -> x1, Pallas kernels: none -> 2.62 us  [settle_outputs(): pl.pallas_call(settle_kernel, grid=(parts,), out_shape=(jax.ShapeDtypeStr...]
where the time goes in v3:
time: 125 us
  Pallas kernels  124 us (99%)
  between operations  1.36 us (1%)
    pallas_call x1, Pallas kernels, streamed(): pl.pallas_call(functools.partial(stream_kernel, n, dps, capacity, block,...  121 us
    pallas_call x1, Pallas kernels, settle_outputs(): pl.pallas_call(settle_kernel, grid=(parts,), out_shape=(jax.ShapeDtypeStr...  2.62 us

profile of v3, /device:TPU:0, one launch (start us, length us, event | category | flops | bytes accessed | tf_op | source)
XLA Modules:
  0.0 125.2 jit_solution(4807306546092766222)
XLA Ops:
  0.6 0.0 copy-start.1
  0.6 0.0 copy-start.3
  0.6 121.2 %shard_map.70 = (bf16[512,2048]{1,0:T(8,128)(2,1)}, s32[1,512]{1,0:T(1,128)S(1)}, s32[1,1]{1,0:T(1,128)}) custom-call(s32[1,512]{1,0:T(1,128)} %bitcast.47, bf16[512,2048]{1,0:T(8,128)(2,1)} %tok_hbm.1, bf16[1,2048,768]{2,1,0:T(8,128)(2,1)} %gate_hbm.1, bf16[1,2048,768]{2,1,0:T(8,128)(2,1)} %up_hbm.1, bf16[1,768,2048]{2,1,0:T(8,128)(2,1)} %down_hbm.1), custom_call_target="tpu_custom_call" | custom-call | tf_op jit(solution)/shard_map/pallas_call | solution.py:1011
  122.5 0.0 copy-done.1
  122.5 0.0 copy-done.3
  122.5 2.6 %conditional.1 = (bf16[512,2048]{1,0:T(8,128)(2,1)}, s32[512]{0:T(512)}) conditional(s32[]{:T(128)} %bitcast.19, (bf16[512,2048]{1,0:T(8,128)(2,1)}, s32[1,512]{1,0:T(1,128)S(1)}) %tuple.23, (s32[512,1]{0,1:T(1,128)S(1)}, bf16[512,2048]{1,0:T(8,128)(2,1)}, bf16[1,2048,768]{2,1,0:T(8,128)(2,1)S(1)}, bf16[1,2048,768]{2,1,0:T(8,128)(2,1)}, ...), branch_computations={%region_0.0_spmd, %region_1.12_spmd} | conditional | flops 13971276800 | bytes 87129008 | solution.py:1045
  122.6 2.6 %branch_0_fun.1 = (bf16[512,2048]{1,0:T(8,128)(2,1)}, s32[1,512]{1,0:T(1,128)}) custom-call(bf16[512,2048]{1,0:T(8,128)(2,1)} %get-tuple-element.46.rows_in, s32[1,512]{1,0:T(1,128)S(1)} %get-tuple-element.47.slot_in), custom_call_target="tpu_custom_call" | custom-call | tf_op jit(solution)/shard_map/cond/branch_0_fun/pallas_call | solution.py:981
Async XLA Ops:
  0.6 121.9 %copy-start.1 = (bf16[1,2048,768]{2,1,0:T(8,128)(2,1)S(1)}, bf16[1,2048,768]{2,1,0:T(8,128)(2,1)}, u32[]{:S(2)}) copy-start(bf16[1,2048,768]{2,1,0:T(8,128)(2,1)} %gate_hbm.1) | copy-start | bytes 9437188
  0.6 121.9 %copy-start.3 = (s32[512,1]{0,1:T(1,128)S(1)}, s32[512,1]{0,1:T(1,128)}, u32[]{:S(2)}) copy-start(s32[512,1]{0,1:T(1,128)} %param.12) | copy-start | bytes 6148

commit v4 on v3

--- a/solution.py
+++ b/solution.py
@@ -351,7 +351,7 @@
 
 
 RUN_ORDER = {
-    "A": ("go op", "go oq", "go oi", "ret op", "ret oq", "ret oi"),
+    "A": ("go oq", "go op", "go oi", "ret op", "ret oq", "ret oi"),
     "M": (
         "go ip", "go iq", "go oq", "go op", "ret ip", "ret op", "ret iq", "ret oq",
     ),
@@ -526,8 +526,8 @@
     zero1 = jnp.zeros((1, 1), jnp.int32)
     to_o = jnp.where(inner, zero1, LOCAL_KEY)
     to_i = jnp.where(inner, LOCAL_KEY, own_rows("p") + own_rows("q"))
-    to_p = jnp.where(inner, zero1 + FAR_KEY, 0)
-    to_q = own_rows("p") + to_p
+    to_p = jnp.where(inner, FAR_KEY, own_rows("q"))
+    to_q = jnp.where(inner, FAR_KEY + own_rows("p"), 0)
     key = jnp.zeros((1, tok), jnp.int32)
     for role, to in (("o", to_o), ("i", to_i), ("p", to_p), ("q", to_q)):
         key = jnp.where(pair_row == roles[role], to + pair_rank, key)
@@ -999,7 +999,7 @@
     capacity = tok * dps
     block = tok // (2 * n)
     far_blocks = 9 * n // 2
-    near_blocks = far_blocks + 1
+    near_blocks = far_blocks
     go_blocks = 13 * n // 4
     back_blocks = n
     blocks = near_blocks

time: 125 us -> 125 us (level)
  no operation moved by 1% of the time
where the time goes in v4:
time: 125 us
  Pallas kernels  123 us (98%)
  between operations  1.36 us (1%)
    pallas_call x1, Pallas kernels, streamed(): pl.pallas_call(functools.partial(stream_kernel, n, dps, capacity, block,...  121 us
    pallas_call x1, Pallas kernels, settle_outputs(): pl.pallas_call(settle_kernel, grid=(parts,), out_shape=(jax.ShapeDtypeStr...  2.62 us

profile of v4, /device:TPU:0, one launch (start us, length us, event | category | flops | bytes accessed | tf_op | source)
XLA Modules:
  0.0 124.6 jit_solution(14715394534948446848)
XLA Ops:
  0.6 0.0 copy-start.1
  0.6 0.0 copy-start.3
  0.6 120.6 %shard_map.70 = (bf16[512,2048]{1,0:T(8,128)(2,1)}, s32[1,512]{1,0:T(1,128)S(1)}, s32[1,1]{1,0:T(1,128)}) custom-call(s32[1,512]{1,0:T(1,128)} %bitcast.47, bf16[512,2048]{1,0:T(8,128)(2,1)} %tok_hbm.1, bf16[1,2048,768]{2,1,0:T(8,128)(2,1)} %gate_hbm.1, bf16[1,2048,768]{2,1,0:T(8,128)(2,1)} %up_hbm.1, bf16[1,768,2048]{2,1,0:T(8,128)(2,1)} %down_hbm.1), custom_call_target="tpu_custom_call" | custom-call | tf_op jit(solution)/shard_map/pallas_call | solution.py:1011
  122.0 0.0 copy-done.1
  122.0 0.0 copy-done.3
  122.0 2.6 %conditional.1 = (bf16[512,2048]{1,0:T(8,128)(2,1)}, s32[512]{0:T(512)}) conditional(s32[]{:T(128)} %bitcast.19, (bf16[512,2048]{1,0:T(8,128)(2,1)}, s32[1,512]{1,0:T(1,128)S(1)}) %tuple.23, (s32[512,1]{0,1:T(1,128)S(1)}, bf16[512,2048]{1,0:T(8,128)(2,1)}, bf16[1,2048,768]{2,1,0:T(8,128)(2,1)S(1)}, bf16[1,2048,768]{2,1,0:T(8,128)(2,1)}, ...), branch_computations={%region_0.0_spmd, %region_1.12_spmd} | conditional | flops 13971276800 | bytes 87129008 | solution.py:1045
  122.0 2.6 %branch_0_fun.1 = (bf16[512,2048]{1,0:T(8,128)(2,1)}, s32[1,512]{1,0:T(1,128)}) custom-call(bf16[512,2048]{1,0:T(8,128)(2,1)} %get-tuple-element.46.rows_in, s32[1,512]{1,0:T(1,128)S(1)} %get-tuple-element.47.slot_in), custom_call_target="tpu_custom_call" | custom-call | tf_op jit(solution)/shard_map/cond/branch_0_fun/pallas_call | solution.py:981
Async XLA Ops:
  0.6 121.3 %copy-start.1 = (bf16[1,2048,768]{2,1,0:T(8,128)(2,1)S(1)}, bf16[1,2048,768]{2,1,0:T(8,128)(2,1)}, u32[]{:S(2)}) copy-start(bf16[1,2048,768]{2,1,0:T(8,128)(2,1)} %gate_hbm.1) | copy-start | bytes 9437188
  0.6 121.3 %copy-start.3 = (s32[512,1]{0,1:T(1,128)S(1)}, s32[512,1]{0,1:T(1,128)}, u32[]{:S(2)}) copy-start(s32[512,1]{0,1:T(1,128)} %param.12) | copy-start | bytes 6148
